TPU v7x, 128 devices: a whole 4x4x4 slice. The times are simulated.
128 devices in a mesh: ep: 16 (over y, z), tp: 8 (over x, core).
Axes of the slice: x: 4, y: 4, z: 4, core: 2. Of those that a mesh axis runs over, the one named last changes fastest.
Arguments:
- tokens: bfloat16 [2048, 4096], P(('ep', 'tp')), may hold values from -6 to 6
- routes: int32 [2048, 2], P(('ep', 'tp')), may hold values from 0 to 15, all different within a row; in each aligned block of 16 rows (0 to 15, 16 to 31, ...) at most 4 rows name the same one
- combine: float32 [2048, 2], P(('ep', 'tp')), may hold values from 0.25 to 1
- gate_weight: bfloat16 [16, 4096, 4096], P('ep', None, 'tp'), may hold values from -0.09375 to 0.09375
- up_weight: bfloat16 [16, 4096, 4096], P('ep', None, 'tp'), may hold values from -0.09375 to 0.09375
- down_weight: bfloat16 [16, 4096, 4096], P('ep', 'tp'), may hold values from -0.09375 to 0.09375
Outputs:
- moe_output: bfloat16 [2048, 4096], P(('ep', 'tp'))
Inputs may be any that keep to these rules, and one draw needn't show every extreme that they name: `routes`: each row names 2 different experts. Among the rows of one device no expert is named more than 4 times, and in every draw some expert is named exactly 4 times by the rows of some device.
All inputs are finite; a program needn't handle non-finite values.
Results may differ from a plain program's by a relative error of at most 0.015.
Values may be sent and summed in bfloat16 or wider, within the bound.
A program may use at most 64 MiB of HBM per device.

v0:
```python
import jax
import jax.numpy as jnp
from jax import lax
from jax.sharding import PartitionSpec as P


def body(tokens, routes, combine, gate_weight, up_weight, down_weight):
    token_rows, feature_width = tokens.shape
    top_count = routes.shape[1]
    experts_here = gate_weight.shape[0]
    rank_count = lax.axis_size("ep")
    groups = lax.axis_size("tp")
    experts_all = experts_here * rank_count
    capacity = 2 * token_rows * top_count // experts_all
    flat_ids = routes.reshape(-1)
    onehot = (flat_ids[:, None] == jnp.arange(experts_all, dtype=jnp.int32)[None, :]).astype(
        jnp.int32
    )
    earlier = jnp.cumsum(onehot, axis=0) - onehot
    slot_index = jnp.sum(earlier * onehot, axis=1)
    target = flat_ids * capacity + slot_index
    selector = (
        target[:, None] == jnp.arange(experts_all * capacity, dtype=jnp.int32)[None, :]
    ).astype(jnp.bfloat16)
    repeated = jnp.repeat(tokens, top_count, axis=0)
    buffer = lax.dot_general(
        selector, repeated, (((0,), (0,)), ((), ())), preferred_element_type=jnp.float32
    ).astype(jnp.bfloat16)
    shaped = buffer.reshape(rank_count, 1, experts_here, capacity, feature_width)
    copies = jnp.broadcast_to(shaped, (rank_count, groups, experts_here, capacity, feature_width))
    copies = copies.reshape(rank_count * groups, experts_here, capacity, feature_width)
    arrived = lax.all_to_all(copies, ("ep", "tp"), split_axis=0, concat_axis=0, tiled=True)
    arrived = arrived.reshape(rank_count, groups, experts_here, capacity, feature_width)
    gate_values = jnp.einsum(
        "abecd,edf->abecf", arrived, gate_weight, preferred_element_type=jnp.float32
    )
    up_values = jnp.einsum(
        "abecd,edf->abecf", arrived, up_weight, preferred_element_type=jnp.float32
    )
    hidden = (jax.nn.silu(gate_values) * up_values).astype(jnp.bfloat16)
    partials = jnp.einsum(
        "abecf,efd->abecd", hidden, down_weight, preferred_element_type=jnp.float32
    )
    summed = lax.psum_scatter(partials.astype(jnp.bfloat16), "tp", scatter_dimension=1, tiled=True)
    returned = lax.all_to_all(summed, "ep", split_axis=0, concat_axis=0, tiled=True)
    returned = returned.reshape(experts_all * capacity, feature_width)
    picked = jnp.dot(selector, returned, preferred_element_type=jnp.float32).reshape(
        token_rows, top_count, feature_width
    )
    return jnp.sum(combine[:, :, None] * picked, axis=1).astype(jnp.bfloat16)


def solution(mesh):
    return jax.shard_map(
        body,
        mesh=mesh,
        in_specs=(
            P(("ep", "tp"), None),
            P(("ep", "tp"), None),
            P(("ep", "tp"), None),
            P("ep", None, "tp"),
            P("ep", None, "tp"),
            P("ep", "tp", None),
        ),
        out_specs=P(("ep", "tp"), None),
        check_vma=False,
    )
```

profile of v0, /device:TPU:0, one launch (start us, length us, event | category | flops | bytes accessed | tf_op | source)
XLA Modules:
  0.0 148.9 jit_solution(17373082179220876680)
XLA Ops:
  6.5 0.0 reduce-scatter.2.cloned.1.call-start
  6.5 0.8 copy.27
  7.3 0.1 eq.50
  7.4 0.1 fusion.34
  7.5 0.1 reduce_window_sum.11
  7.5 0.2 select_reduce_fusion
  7.7 1.1 broadcast_in_dim.16
  8.8 0.1 reshape.73
  8.9 0.4 convolution_convert_fusion.1
  9.3 0.2 broadcast_in_dim.17
  9.5 2.1 %broadcast_in_dim.18 = bf16[16,8,4,4096]{3,2,1,0:T(4,128)(2,1)S(1)} broadcast(bf16[16,4,4096]{2,1,0:T(4,128)(2,1)S(1)} %broadcast_in_dim.17), dimensions={0,2,3} | broadcast | bytes 4718592 | tf_op jit(solution)/shard_map/broadcast_in_dim | solution.py:30
  11.7 0.0 copy-start.2
  11.7 63.8 %all_to_all.10 = bf16[128,1,4,4096]{3,2,1,0:T(4,128)(2,1)S(1)} all-to-all(bf16[128,1,4,4096]{3,2,1,0:T(4,128)(2,1)S(1)} %bitcast.70), channel_id=1, replica_groups=mesh['ep'=16,'tp'=8] {'ep','tp'}, dimensions={0} | all-to-all | bytes 8388608 | tf_op jit(solution)/shard_map/all_to_all | solution.py:32
  75.5 0.0 copy-done.2
  75.5 0.0 copy-start.3
  75.5 2.6 %fusion.8 = f32[16,8,1,4,512]{4,1,3,0,2:T(8,128)S(1)} fusion(bf16[1,4096,512]{2,1,0:T(8,128)(2,1)S(1)} %copy-done.2, bf16[128,1,4,4096]{3,2,1,0:T(4,128)(2,1)S(1)} %all_to_all.10), kind=kOutput, calls=%fused_computation.12 | convolution fusion | flops 2147483648 | bytes 9437184 | tf_op jit(solution)/shard_map/abecd,edf->abecf/dot_general | solution.py:34
  78.1 0.0 copy-done.3
  78.1 0.0 copy-start.4
  78.1 2.7 %fusion.28 = bf16[16,8,4,512]{3,1,2,0:T(8,128)(2,1)S(1)} fusion(bf16[1,4096,512]{2,1,0:T(8,128)(2,1)S(1)} %copy-done.3, f32[16,8,1,4,512]{4,1,3,0,2:T(8,128)S(1)} %fusion.8, bf16[128,1,4,4096]{3,2,1,0:T(4,128)(2,1)S(1)} %all_to_all.10), kind=kOutput, calls=%fused_computation.16 | convolution fusion | flops 2149056512 | bytes 9961472 | tf_op jit(solution)/shard_map/abecd,edf->abecf/dot_general | solution.py:37
  80.8 0.0 copy-done.4
  80.8 2.4 %fusion = bf16[16,8,1,4,4096]{4,1,3,0,2:T(8,128)(2,1)S(1)} fusion(bf16[16,8,4,512]{3,1,2,0:T(8,128)(2,1)S(1)} %fusion.28, bf16[1,512,4096]{2,1,0:T(8,128)(2,1)S(1)} %copy-done.4), kind=kOutput, calls=%fused_computation.1 | convolution fusion | flops 2149580800 | bytes 8912896 | tf_op jit(solution)/shard_map/abecf,efd->abecd/dot_general | solution.py:41
  83.2 4.2 %copy.32 = bf16[16,8,1,4,4096]{4,0,3,2,1:T(8,128)(2,1)} copy(bf16[16,8,1,4,4096]{4,1,3,0,2:T(8,128)(2,1)S(1)} %fusion) | data formatting | bytes 8388608 | tf_op jit(solution)/shard_map/convert_element_type | solution.py:44
  87.4 0.0 copy-start
  87.4 0.0 copy-start.1
  87.4 0.0 reduce-scatter.2.cloned.1.call-update
  87.4 34.2 %reduce-scatter.2.cloned.1.call-done = bf16[16,1,1,4,4096]{4,0,3,2,1:T(8,128)(2,1)} async-done(((bf16[16,8,1,4,4096]{4,0,3,2,1:T(8,128)(2,1)}), bf16[16,1,1,4,4096]{4,0,3,2,1:T(8,128)(2,1)}) %reduce-scatter.2.cloned.1.call-update) | async-done | bytes 524304 | tf_op jit(solution)/shard_map/reduce_scatter | solution.py:44
  121.6 2.2 %copy.33 = bf16[16,1,1,4,4096]{4,3,2,1,0:T(4,128)(2,1)} copy(bf16[16,1,1,4,4096]{4,0,3,2,1:T(8,128)(2,1)} %reduce-scatter.2.cloned.1.call-done) | data formatting | bytes 1048576 | tf_op jit(solution)/shard_map/reduce_scatter | solution.py:44
  123.9 7.0 %all-to-all-start.1 = ((bf16[16,1,1,4,4096]{4,3,2,1,0:T(4,128)(2,1)}), bf16[16,1,1,4,4096]{4,3,2,1,0:T(4,128)(2,1)S(1)}, u32[]{:S(2)}, u32[]{:S(2)}) async-start(bf16[16,1,1,4,4096]{4,3,2,1,0:T(4,128)(2,1)} %copy.33), calls=%async_computation.2 | async-start | bytes 1048576 | tf_op jit(solution)/shard_map/all_to_all | solution.py:45
  130.9 0.1 reduce_sum.21
  131.0 0.1 copy.28
  131.1 0.0 copy-done
  131.1 9.9 %all-to-all-done.1 = bf16[16,1,1,4,4096]{4,3,2,1,0:T(4,128)(2,1)S(1)} async-done(((bf16[16,1,1,4,4096]{4,3,2,1,0:T(4,128)(2,1)}), bf16[16,1,1,4,4096]{4,3,2,1,0:T(4,128)(2,1)S(1)}, u32[]{:S(2)}, u32[]{:S(2)}) %all-to-all-start.1) | async-done | bytes 524320 | tf_op jit(solution)/shard_map/all_to_all | solution.py:45
  141.0 0.1 reshape.83
  141.1 0.0 copy-done.1
  141.1 0.9 fusion.33
  (2 shorter events, 0.0 us)
Async XLA Ops:
  6.5 115.1 %reduce-scatter.2.cloned.1.call-start = ((), (), s32[]{:S(2)}) async-start(), calls=%async_computation.3 | async-start | bytes 4718592 | tf_op jit(solution)/shard_map/reduce_scatter | solution.py:44
  11.7 63.8 %copy-start.2 = (bf16[1,4096,512]{2,1,0:T(8,128)(2,1)S(1)}, bf16[1,4096,512]{2,1,0:T(8,128)(2,1)}, u32[]{:S(2)}) copy-start(bf16[1,4096,512]{2,1,0:T(8,128)(2,1)} %param.9) | copy-start | bytes 12582916
  75.5 2.6 %copy-start.3 = (bf16[1,4096,512]{2,1,0:T(8,128)(2,1)S(1)}, bf16[1,4096,512]{2,1,0:T(8,128)(2,1)}, u32[]{:S(2)}) copy-start(bf16[1,4096,512]{2,1,0:T(8,128)(2,1)} %param.10) | copy-start | bytes 12582916
  78.1 2.7 %copy-start.4 = (bf16[1,512,4096]{2,1,0:T(8,128)(2,1)S(1)}, bf16[1,512,4096]{2,1,0:T(8,128)(2,1)}, u32[]{:S(2)}) copy-start(bf16[1,512,4096]{2,1,0:T(8,128)(2,1)} %param.11) | copy-start | bytes 12582916
  87.4 43.6 %copy-start = (s32[16,2]{0,1:T(2,128)S(1)}, s32[16,2]{0,1:T(2,128)}, u32[]{:S(2)}) copy-start(s32[16,2]{0,1:T(2,128)} %param.7) | copy-start | bytes 388
  87.4 53.7 %copy-start.1 = (f32[16,2]{0,1:T(2,128)S(1)}, f32[16,2]{0,1:T(2,128)}, u32[]{:S(2)}) copy-start(f32[16,2]{0,1:T(2,128)} %param.8) | copy-start | bytes 388
  123.9 17.1 %all-to-all-start.1 = ((bf16[16,1,1,4,4096]{4,3,2,1,0:T(4,128)(2,1)}), bf16[16,1,1,4,4096]{4,3,2,1,0:T(4,128)(2,1)S(1)}, u32[]{:S(2)}, u32[]{:S(2)}) async-start(bf16[16,1,1,4,4096]{4,3,2,1,0:T(4,128)(2,1)} %copy.33), calls=%async_computation.2 | async-start | bytes 1048576 | tf_op jit(solution)/shard_map/all_to_all | solution.py:45
Sparse Core Ops, SparseCore 0:
  87.6 34.0 reduce-scatter.1
where the time goes:
time: 149 us
  blocking collectives  63.8 us (43%)
  waiting for transfers between devices  44.1 us (30%)
  between operations  13.5 us (9%)
  local copies, waits for them, and re-layouts  11.1 us (7%)
  matrix products  8.99 us (6%)
  starting transfers between devices  7.02 us (5%)
    all_to_all x1, blocking collectives, body(): lax.all_to_all(copies, ('ep', 'tp'), split_axis=0, concat_axis=0, tiled=T...  63.8 us
    reduce_scatter x1, waiting for transfers between devices, body(): lax.psum_scatter(partials.astype(jnp.bfloat16), 'tp', scatter_dimension=1...  34.2 us
    all_to_all x1, waiting for transfers between devices, body(): lax.all_to_all(summed, 'ep', split_axis=0, concat_axis=0, tiled=True)  9.92 us
    all_to_all x1, starting transfers between devices, body(): lax.all_to_all(summed, 'ep', split_axis=0, concat_axis=0, tiled=True)  7.02 us
    convert_element_type x1, local copies, waits for them, and re-layouts, body(): partials.astype(jnp.bfloat16)  4.22 us
  transfers between devices with their start and end apart: 2, of which 2 were waited for; matrix products, arithmetic and copies ran while one was open for 0% of the time, Pallas kernels for 0%

commit v1 on v0

v1 whole, which is shorter than its diff:
```python
import jax
import jax.numpy as jnp
from jax import lax
from jax.experimental import pallas as pl
from jax.experimental.pallas import tpu as pltpu
from jax.sharding import PartitionSpec as P

MESH = pl.DeviceIdType.MESH
F32 = jnp.float32
BF16 = jnp.bfloat16
CW = 512
NY = 4
NZ = 4
NX = 4
IN_ORDER = (0, 1, 3, 2)
OUT_ORDER = (2, 1, 3, 0)
Z_ORDER = (2, 1, 3, 0)


def kernel(
    tok_ref, info_ref, wg_hbm, wu_hbm, wd_hbm, out_ref,
    tr, infos, pk, xs, wg, wu, wd, accg, accu, hid, sel, whi, wlo,
    ds, dr, q, sa, ra, sb, rb, s1p, r1m, s1m, r1p, fin, ret, osl, outr,
    w_sem, t_send, t_recv, i_send, i_recv, a_send, a_recv,
    g_send, g_recv, d_send, d_recv, r_send, r_recv, b_send, b_recv, o_send, o_recv,
):
    ep = lax.axis_index("ep")
    tp = lax.axis_index("tp")
    y, z = ep // NZ, ep % NZ
    x, c = tp // 2, tp % 2

    def on_tp(other):
        return {"ep": ep, "tp": other}

    def on_ep(other):
        return {"ep": other, "tp": tp}

    def remote(src, dst, send_sem, recv_sem, device):
        copy = pltpu.make_async_remote_copy(
            src_ref=src, dst_ref=dst, send_sem=send_sem, recv_sem=recv_sem,
            device_id=device, device_id_type=MESH,
        )
        copy.start()
        return copy

    loads = []
    for n, (src, dst) in enumerate(((wg_hbm, wg), (wu_hbm, wu), (wd_hbm, wd))):
        load = pltpu.make_async_copy(src, dst, w_sem.at[n])
        load.start()
        loads.append(load)

    barrier = pltpu.get_barrier_semaphore()
    for j in range(1, 8):
        pl.semaphore_signal(barrier, inc=1, device_id=on_tp((tp + j) % 8), device_id_type=MESH)
    for dy in range(NY):
        for dz in range(NZ):
            if dy or dz:
                other = ((y + dy) % NY) * NZ + (z + dz) % NZ
                pl.semaphore_signal(barrier, inc=1, device_id=on_ep(other), device_id_type=MESH)
    pl.semaphore_wait(barrier, 22)

    sent = []
    first = []
    for j in range(1, 8):
        other = (tp + j) % 8
        first.append(remote(info_ref, infos.at[tp], i_send.at[j], i_recv.at[j], on_tp(other)))
    for j in range(1, 8):
        other = (tp + j) % 8
        cols = pl.ds(pl.multiple_of(other * CW, CW), CW)
        first.append(remote(tok_ref.at[:, cols], tr.at[tp], t_send.at[j], t_recv.at[j], on_tp(other)))
    infos[tp] = info_ref[...]
    tr[tp] = tok_ref[:, pl.ds(pl.multiple_of(tp * CW, CW), CW)]
    for copy in first[:7]:
        copy.wait_recv()
    sent += first

    lane8 = lax.broadcasted_iota(jnp.int32, (8, 128), 1) // 16
    info = jnp.zeros((8, 128), F32)
    for b in range(8):
        info = info + jnp.where(lane8 == b, infos[b], 0.0)
    row = lax.broadcasted_iota(jnp.int32, (512, 128), 0)
    lane = lax.broadcasted_iota(jnp.int32, (512, 128), 1)
    expert = (row // 32).astype(F32)
    slot = (row % 4).astype(F32)
    same = (lane // 16) == ((row % 32) // 4)
    first_of = jnp.where(info[0:1] == expert, 1.0, 0.0)
    second_of = jnp.where(info[1:2] == expert, 1.0, 0.0)
    named = first_of + second_of
    urow = lax.broadcasted_iota(jnp.int32, (128, 128), 0)
    ulane = lax.broadcasted_iota(jnp.int32, (128, 128), 1)
    before = jnp.where((urow < ulane) & ((urow // 16) == (ulane // 16)), 1.0, 0.0).astype(BF16)
    count = jnp.dot(named.astype(BF16), before, preferred_element_type=F32)
    hit = same & (count == slot)
    sel[...] = jnp.where(hit, named, 0.0).astype(BF16)
    weight = jnp.where(hit, first_of * info[2:3] + second_of * info[3:4], 0.0)
    weight = weight.T
    high = weight.astype(BF16)
    whi[...] = high
    wlo[...] = (weight - high.astype(F32)).astype(BF16)

    for copy in first[7:]:
        copy.wait_recv()
    picked = jnp.dot(sel[...], tr[...].reshape(128, CW), preferred_element_type=F32)
    pk[...] = picked.astype(BF16).reshape(16, 32, CW)
    xs[tp, ep] = pk[ep]

    spread = {}
    for dy in IN_ORDER:
        for dz in Z_ORDER:
            if dy or dz:
                other = ((y + dy) % NY) * NZ + (z + dz) % NZ
                k = dy * NZ + dz
                spread[dy, dz] = remote(
                    pk.at[other], xs.at[tp, ep], a_send.at[k], a_recv.at[k], on_ep(other)
                )
    sent += list(spread.values())

    mate = x * 2 + (1 - c)
    right = ((x + 1) % NX) * 2 + c
    left = ((x + 3) % NX) * 2 + c
    far = ((x + 2) % NX) * 2 + c

    to_mate, to_right, to_left = [], [], []
    for i, dy in enumerate(IN_ORDER):
        for dz in range(NZ):
            if dy or dz:
                spread[dy, dz].wait_recv()
        ys = ((y + NY - dy) % NY) * NZ
        block = xs.at[tp, pl.ds(ys, 4)]
        to_right.append(remote(block, block, g_send.at[0, i], g_recv.at[0, i], on_tp(right)))
        to_left.append(remote(block, block, g_send.at[1, i], g_recv.at[1, i], on_tp(left)))
        to_mate.append(remote(block, block, g_send.at[2, i], g_recv.at[2, i], on_tp(mate)))
    sent += to_right + to_left + to_mate
    loads[0].wait()
    loads[1].wait()
    for copy in to_mate:
        copy.wait_recv()

    def gate_up(chip, fresh):
        gate = up = None
        for core in range(2):
            t = chip * 2 + core
            a = xs[t].reshape(512, CW)
            rows = pl.ds(pl.multiple_of(t * CW, CW), CW)
            g1 = jnp.dot(a, wg[rows, :], preferred_element_type=F32)
            u1 = jnp.dot(a, wu[rows, :], preferred_element_type=F32)
            gate = g1 if gate is None else gate + g1
            up = u1 if up is None else up + u1
        if fresh:
            accg[...] = gate
            accu[...] = up
        else:
            accg[...] += gate
            accu[...] += up

    gate_up(x, True)

    on_right, on_left, mate_left, mate_right = [], [], [], []
    for i, dy in enumerate(IN_ORDER):
        ys = ((y + NY - dy) % NY) * NZ
        to_right[i].wait_recv()
        half = xs.at[left, pl.ds(ys, 2)]
        on_right.append(remote(half, half, g_send.at[3, i], g_recv.at[3, i], on_tp(right)))
        block = xs.at[left, pl.ds(ys, 4)]
        mate_left.append(remote(block, block, g_send.at[5, i], g_recv.at[5, i], on_tp(mate)))
        to_left[i].wait_recv()
        half = xs.at[right, pl.ds(ys + 2, 2)]
        on_left.append(remote(half, half, g_send.at[4, i], g_recv.at[4, i], on_tp(left)))
        block = xs.at[right, pl.ds(ys, 4)]
        mate_right.append(remote(block, block, g_send.at[6, i], g_recv.at[6, i], on_tp(mate)))
    sent += on_right + on_left + mate_left + mate_right
    for copy in mate_left:
        copy.wait_recv()
    gate_up((x + 3) % NX, False)
    mate_far = []

    def pass_far(i):
        ys = ((y + NY - IN_ORDER[i]) % NY) * NZ
        on_right[i].wait_recv()
        half = xs.at[far, pl.ds(ys, 2)]
        mate_far.append(remote(half, half, g_send.at[7, i], g_recv.at[7, i], on_tp(mate)))
        on_left[i].wait_recv()
        half = xs.at[far, pl.ds(ys + 2, 2)]
        mate_far.append(remote(half, half, g_send.at[8, i], g_recv.at[8, i], on_tp(mate)))

    pass_far(0)
    pass_far(1)
    for copy in mate_right:
        copy.wait_recv()
    gate_up((x + 1) % NX, False)
    pass_far(2)
    pass_far(3)
    sent += mate_far
    for copy in mate_far:
        copy.wait_recv()
    gate_up((x + 2) % NX, False)

    gate = accg[...]
    hid[...] = (gate / (1.0 + jnp.exp(-gate)) * accu[...]).astype(BF16)
    loads[2].wait()

    pair = {}

    def down(k):
        chip = (x + k) % NX
        for own in (False, True):
            t = chip * 2 + (c if own else 1 - c)
            cols = pl.ds(pl.multiple_of(t * CW, CW), CW)
            part = jnp.dot(hid[...], wd[:, cols], preferred_element_type=F32)
            part = part.astype(BF16).reshape(16, 32, CW)
            if own:
                q[k] = part
            else:
                ds[k] = part
                pair[k] = remote(ds.at[k], dr.at[k], d_send.at[k], d_recv.at[k], on_tp(mate))

    def chip_sum(k, start, size):
        rows = pl.ds(start, size)
        return q[k, rows].astype(F32) + dr[k, rows].astype(F32)

    down(2)
    down(1)
    pair[2].wait_recv()
    far_right, far_left = [], []
    for i, dy in enumerate(OUT_ORDER):
        yd = ((y + dy) % NY) * NZ
        sa[i] = chip_sum(2, yd, 2).astype(BF16)
        far_right.append(remote(sa.at[i], ra.at[i], r_send.at[0, i], r_recv.at[0, i], on_tp(right)))
        sb[i] = chip_sum(2, yd + 2, 2).astype(BF16)
        far_left.append(remote(sb.at[i], rb.at[i], r_send.at[1, i], r_recv.at[1, i], on_tp(left)))
    down(3)
    down(0)
    sent += list(pair.values()) + far_right + far_left
    pair[1].wait_recv()
    pair[3].wait_recv()
    near = [[], [], [], []]
    for i, dy in enumerate(OUT_ORDER):
        yd = ((y + dy) % NY) * NZ
        s1p[i, 1] = chip_sum(1, yd + 2, 2).astype(BF16)
        near[0].append(remote(s1p.at[i, 1], r1m.at[i, 1], r_send.at[2, i], r_recv.at[2, i], on_tp(right)))
        s1m[i, 0] = chip_sum(3, yd, 2).astype(BF16)
        near[1].append(remote(s1m.at[i, 0], r1p.at[i, 0], r_send.at[3, i], r_recv.at[3, i], on_tp(left)))
        far_right[i].wait_recv()
        s1p[i, 0] = (chip_sum(1, yd, 2) + ra[i].astype(F32)).astype(BF16)
        near[2].append(remote(s1p.at[i, 0], r1m.at[i, 0], r_send.at[4, i], r_recv.at[4, i], on_tp(right)))
        far_left[i].wait_recv()
        s1m[i, 1] = (chip_sum(3, yd + 2, 2) + rb[i].astype(F32)).astype(BF16)
        near[3].append(remote(s1m.at[i, 1], r1p.at[i, 1], r_send.at[5, i], r_recv.at[5, i], on_tp(left)))
    for copies in near:
        sent += copies
    pair[0].wait_recv()
    back = []
    for i, dy in enumerate(OUT_ORDER):
        yd = ((y + dy) % NY) * NZ
        for copies in near:
            copies[i].wait_recv()
        total = chip_sum(0, yd, 4)
        total = total + r1m[i].astype(F32).reshape(4, 32, CW)
        total = total + r1p[i].astype(F32).reshape(4, 32, CW)
        fin[pl.ds(yd, 4)] = total.astype(BF16)
        for dz in Z_ORDER:
            other = yd + (z + dz) % NZ
            if dy or dz:
                k = dy * NZ + dz
                back.append(remote(fin.at[other], ret.at[ep], b_send.at[k], b_recv.at[k], on_ep(other)))
    ret[ep] = fin[ep]
    sent += back
    for copy in back:
        copy.wait_recv()
    rows = ret[...].reshape(512, CW)
    result = jnp.dot(whi[...], rows, preferred_element_type=F32)
    result = result + jnp.dot(wlo[...], rows, preferred_element_type=F32)
    osl[...] = result.astype(BF16).reshape(8, 16, CW)
    outs = []
    for j in range(1, 8):
        other = (tp + j) % 8
        outs.append(remote(osl.at[other], outr.at[tp], o_send.at[j], o_recv.at[j], on_tp(other)))
    outr[tp] = osl[tp]
    sent += outs
    for copy in outs:
        copy.wait_recv()
    for t in range(8):
        out_ref[:, t * CW:(t + 1) * CW] = outr[t]
    for copy in sent:
        copy.wait_send()


def body(tokens, routes, combine, gate_weight, up_weight, down_weight):
    info = jnp.concatenate([routes.astype(F32).T, combine.T, jnp.zeros((4, 16), F32)], axis=0)
    info = jnp.tile(info, (1, 8))
    vmem = pl.BlockSpec(memory_space=pltpu.VMEM)
    hbm = pl.BlockSpec(memory_space=pltpu.HBM)
    dma = pltpu.SemaphoreType.DMA
    part = (16, 32, CW)
    return pl.pallas_call(
        kernel,
        out_shape=jax.ShapeDtypeStruct((16, 4096), BF16),
        in_specs=[vmem, vmem, hbm, hbm, hbm],
        out_specs=vmem,
        scratch_shapes=[
            pltpu.VMEM((8, 16, CW), BF16),
            pltpu.VMEM((8, 8, 128), F32),
            pltpu.VMEM(part, BF16),
            pltpu.VMEM((8,) + part, BF16),
            pltpu.VMEM((4096, 512), BF16),
            pltpu.VMEM((4096, 512), BF16),
            pltpu.VMEM((512, 4096), BF16),
            pltpu.VMEM((512, 512), F32),
            pltpu.VMEM((512, 512), F32),
            pltpu.VMEM((512, 512), BF16),
            pltpu.VMEM((512, 128), BF16),
            pltpu.VMEM((128, 512), BF16),
            pltpu.VMEM((128, 512), BF16),
            pltpu.VMEM((4,) + part, BF16),
            pltpu.VMEM((4,) + part, BF16),
            pltpu.VMEM((4,) + part, BF16),
            pltpu.VMEM((4, 2, 32, CW), BF16),
            pltpu.VMEM((4, 2, 32, CW), BF16),
            pltpu.VMEM((4, 2, 32, CW), BF16),
            pltpu.VMEM((4, 2, 32, CW), BF16),
            pltpu.VMEM((4, 2, 2, 32, CW), BF16),
            pltpu.VMEM((4, 2, 2, 32, CW), BF16),
            pltpu.VMEM((4, 2, 2, 32, CW), BF16),
            pltpu.VMEM((4, 2, 2, 32, CW), BF16),
            pltpu.VMEM(part, BF16),
            pltpu.VMEM(part, BF16),
            pltpu.VMEM((8, 16, CW), BF16),
            pltpu.VMEM((8, 16, CW), BF16),
            dma((3,)),
            dma((8,)), dma((8,)), dma((8,)), dma((8,)),
            dma((16,)), dma((16,)),
            dma((9, 4)), dma((9, 4)),
            dma((4,)), dma((4,)),
            dma((6, 4)), dma((6, 4)),
            dma((16,)), dma((16,)),
            dma((8,)), dma((8,)),
        ],
        compiler_params=pltpu.CompilerParams(
            collective_id=0, has_side_effects=True, vmem_limit_bytes=60 * 1024 * 1024
        ),
        name="moe",
    )(tokens, info, gate_weight[0], up_weight[0], down_weight[0])


def solution(mesh):
    return jax.shard_map(
        body,
        mesh=mesh,
        in_specs=(
            P(("ep", "tp"), None),
            P(("ep", "tp"), None),
            P(("ep", "tp"), None),
            P("ep", None, "tp"),
            P("ep", None, "tp"),
            P("ep", "tp", None),
        ),
        out_specs=P(("ep", "tp"), None),
        check_vma=False,
    )
```

time: 149 us -> 78.5 us (0.53)
  the two profiles are of different devices: /device:TPU:0 before, /device:TPU:1 now
where the time goes in v1:
time: 78.5 us; the launch traced here: 78.3 us
  Pallas kernels  74.5 us (95%)
  local copies, waits for them, and re-layouts  2.32 us (3%)
  other arithmetic  1.43 us (2%)
    pallas_call x1, Pallas kernels, body(): pl.pallas_call(kernel, out_shape=jax.ShapeDtypeStruct((16, 4096), BF16),...  74.5 us

profile of v1, /device:TPU:1, one launch (start us, length us, event | category | flops | bytes accessed | tf_op | source)
XLA Modules:
  0.0 78.3 jit_solution(4330238435401191075)
XLA Ops:
  0.0 0.1 pad.2.clone
  0.1 0.7 convert_bitcast_fusion
  0.8 0.7 maximum_maximum_fusion
  1.5 0.7 tile.10.info_ref
  2.2 74.5 %moe.1 = bf16[16,4096]{1,0:T(8,128)(2,1)} custom-call(bf16[16,4096]{1,0:T(8,128)(2,1)} %tok_ref.1, f32[8,128]{1,0:T(8,128)} %tile.10.info_ref, bf16[4096,512]{1,0:T(8,128)(2,1)} %bitcast.6, bf16[4096,512]{1,0:T(8,128)(2,1)} %bitcast.7, bf16[512,4096]{1,0:T(8,128)(2,1)} %bitcast.8), custom_call_target="tpu_custom_call" | custom-call | tf_op jit(solution)/shard_map/moe/pallas_call | solution.py:295
  76.7 1.6 %copy.8 = bf16[16,4096]{1,0:T(8,128)(2,1)} copy(bf16[16,4096]{1,0:T(8,128)(2,1)} %moe.1) | data formatting | bytes 262144
  (2 shorter events, 0.0 us)

commit v2 on v0

v2 whole, which is shorter than its diff:
```python
import contextlib

import jax
import jax.numpy as jnp
from jax import lax
from jax.experimental import pallas as pl
from jax.experimental.pallas import tpu as pltpu
from jax.sharding import PartitionSpec as P

MESH = pl.DeviceIdType.MESH
PROFILE = False
F32 = jnp.float32
BF16 = jnp.bfloat16
NX, NY, NZ = 4, 4, 4
RW = 384
DW = 512
DIRECT = 8 * RW
HOPS = (
    (0, 0), (1, 1), (3, 3), (0, 2), (2, 2), (1, 3), (3, 1), (2, 0),
    (0, 1), (0, 3), (1, 0), (3, 0), (1, 2), (3, 2), (2, 1), (2, 3),
)
COPIES = 176


def scope(name):
    return jax.named_scope(name) if PROFILE else contextlib.nullcontext()


def kernel(
    tok_ref, info_ref, wg_hbm, wu_hbm, wd_hbm, out_ref,
    infos, t2, t1, p2, p1, x2, x1, wg, wu, wd, accg, accu, hid, sel, whi, wlo,
    part2, mate2, part1, mate1, far_s, far_r, near_s, near_r,
    fin2, fin1, r2, r1, o2s, o1s, o2r, o1r,
    w_sem, send_sems, recv_sems,
):
    ep = lax.axis_index("ep")
    tp = lax.axis_index("tp")
    y, z = ep // NZ, ep % NZ
    x, c = tp // 2, tp % 2
    sent = []

    def on_tp(other):
        return {"ep": ep, "tp": other}

    def on_ep(other):
        return {"ep": other, "tp": tp}

    def remote(src, dst, device):
        k = len(sent)
        copy = pltpu.make_async_remote_copy(
            src_ref=src, dst_ref=dst, send_sem=send_sems.at[k], recv_sem=recv_sems.at[k],
            device_id=device, device_id_type=MESH,
        )
        copy.start()
        sent.append(copy)
        return copy

    def arrived(copies):
        for copy in copies:
            copy.wait_recv()

    mate = x * 2 + (1 - c)
    right = ((x + 1) % NX) * 2 + c
    left = ((x + 3) % NX) * 2 + c
    far = ((x + 2) % NX) * 2 + c

    with scope("k00_barrier"):
        loads = []
        for n, (src, dst) in enumerate(((wg_hbm, wg), (wu_hbm, wu), (wd_hbm, wd))):
            load = pltpu.make_async_copy(src, dst, w_sem.at[n])
            load.start()
            loads.append(load)
        barrier = pltpu.get_barrier_semaphore()
        for j in range(1, 8):
            pl.semaphore_signal(barrier, inc=1, device_id=on_tp((tp + j) % 8), device_id_type=MESH)
        for dy in range(NY):
            for dz in range(NZ):
                if dy or dz:
                    other = ((y + dy) % NY) * NZ + (z + dz) % NZ
                    pl.semaphore_signal(barrier, inc=1, device_id=on_ep(other), device_id_type=MESH)
        pl.semaphore_wait(barrier, 22)

    def ring_cols(t):
        return pl.ds(pl.multiple_of(t * RW, 128), RW)

    def direct_cols(core):
        return pl.ds(pl.multiple_of(DIRECT + core * DW, 128), DW)

    with scope("k01_tsend"):
        offsets = (4, 5, 3, 2, 6, 7, 1)
        peers = [(tp + j) % 8 for j in offsets]
        got_info = [remote(info_ref, infos.at[tp], on_tp(t)) for t in peers]
        got_t2 = [remote(tok_ref.at[:, ring_cols(t)], t2.at[tp], on_tp(t)) for t in peers]
        got_t1 = [remote(tok_ref.at[:, direct_cols(t % 2)], t1.at[tp], on_tp(t)) for t in peers]
        infos[tp] = info_ref[...]
        t2[tp] = tok_ref[:, ring_cols(tp)]
        t1[tp] = tok_ref[:, direct_cols(c)]
    with scope("k02_iwait"):
        arrived(got_info)

    with scope("k03_sel"):
        lane8 = lax.broadcasted_iota(jnp.int32, (8, 128), 1) // 16
        info = jnp.zeros((8, 128), F32)
        for b in range(8):
            info = info + jnp.where(lane8 == b, infos[b], 0.0)
        row = lax.broadcasted_iota(jnp.int32, (512, 128), 0)
        lane = lax.broadcasted_iota(jnp.int32, (512, 128), 1)
        expert = (row // 32).astype(F32)
        slot = (row % 4).astype(F32)
        same = (lane // 16) == ((row % 32) // 4)
        first_of = jnp.where(info[0:1] == expert, 1.0, 0.0)
        second_of = jnp.where(info[1:2] == expert, 1.0, 0.0)
        named = first_of + second_of
        urow = lax.broadcasted_iota(jnp.int32, (128, 128), 0)
        ulane = lax.broadcasted_iota(jnp.int32, (128, 128), 1)
        before = jnp.where((urow < ulane) & ((urow // 16) == (ulane // 16)), 1.0, 0.0).astype(BF16)
        count = jnp.dot(named.astype(BF16), before, preferred_element_type=F32)
        hit = same & (count == slot)
        sel[...] = jnp.where(hit, named, 0.0).astype(BF16)

    with scope("k04_twait"):
        arrived(got_t2)

    def spread(picked, landing):
        copies = {}
        for n in (4, 1, 2, 3, 5, 6, 7, 12, 13, 14, 15, 8, 9, 10, 11):
            dy, dz = HOPS[n]
            other = ((y + dy) % NY) * NZ + (z + dz) % NZ
            copies[n] = remote(picked.at[other], landing.at[n // 8, n % 8], on_ep(other))
        return copies

    def of_half(copies, h):
        return [copy for n, copy in copies.items() if n // 8 == h]

    with scope("k05_pick2"):
        picked = jnp.dot(sel[...], t2[...].reshape(128, RW), preferred_element_type=F32)
        p2[...] = picked.astype(BF16).reshape(16, 32, RW)
        x2[tp, 0, 0] = p2[ep]
        spread2 = spread(p2, x2.at[tp])
    with scope("k06_pick1"):
        arrived(got_t1)
        picked = jnp.dot(sel[...], t1[...].reshape(128, DW), preferred_element_type=F32)
        p1[...] = picked.astype(BF16).reshape(16, 32, DW)
        x1[c, 0, 0] = p1[ep]
    with scope("k07_weights"):
        weight = jnp.where(hit, first_of * info[2:3] + second_of * info[3:4], 0.0).T
        high = weight.astype(BF16)
        whi[...] = high
        wlo[...] = (weight - high.astype(F32)).astype(BF16)

    LO, HI, ALL = pl.ds(0, 4), pl.ds(4, 4), pl.ds(0, 8)

    def push(t, h, rows, device):
        block = x2.at[t, h, rows]
        return remote(block, block, on_tp(device))

    def half_state():
        return {}

    st = [half_state(), half_state()]

    def own_first(h):
        s = st[h]
        s["r_lo"] = push(tp, h, LO, right)
        s["l_hi"] = push(tp, h, HI, left)
        s["m_own"] = push(tp, h, ALL, mate)

    def own_second(h):
        s = st[h]
        s["r_hi"] = push(tp, h, HI, right)
        s["l_lo"] = push(tp, h, LO, left)

    def forward(h):
        s = st[h]
        s["r_lo"].wait_recv()
        s["f_lo"] = push(left, h, LO, right)
        s["m_left_lo"] = push(left, h, LO, mate)
        s["l_hi"].wait_recv()
        s["f_hi"] = push(right, h, HI, left)
        s["m_right_hi"] = push(right, h, HI, mate)

    def near_rest(h):
        s = st[h]
        s["r_hi"].wait_recv()
        s["m_left_hi"] = push(left, h, HI, mate)
        s["l_lo"].wait_recv()
        s["m_right_lo"] = push(right, h, LO, mate)

    def far_rest(h):
        s = st[h]
        s["f_lo"].wait_recv()
        s["m_far_lo"] = push(far, h, LO, mate)
        s["f_hi"].wait_recv()
        s["m_far_hi"] = push(far, h, HI, mate)

    spread1 = {}

    def direct_share(h):
        arrived(of_half(spread1, h))
        block = x1.at[c, h]
        st[h]["m_direct"] = remote(block, block, on_tp(mate))

    def accumulate(h, a, rows, fresh):
        gate = jnp.dot(a, wg[rows, :], preferred_element_type=F32)
        up = jnp.dot(a, wu[rows, :], preferred_element_type=F32)
        if fresh:
            accg[h] = gate
            accu[h] = up
        else:
            accg[h] += gate
            accu[h] += up

    def gate_up(h, k, names):
        arrived([st[h][name] for name in names])
        chip = (x + k) % NX
        a = jnp.concatenate(
            [x2[chip * 2, h].reshape(256, RW), x2[chip * 2 + 1, h].reshape(256, RW)], axis=1
        )
        accumulate(h, a, pl.ds(pl.multiple_of(chip * 2 * RW, 256), 2 * RW), k == 0)

    def gate_up_direct(h):
        st[h]["m_direct"].wait_recv()
        a = jnp.concatenate([x1[0, h].reshape(256, DW), x1[1, h].reshape(256, DW)], axis=1)
        accumulate(h, a, pl.ds(DIRECT, 2 * DW), False)

    def silu(h):
        gate = accg[h]
        hid[h] = (gate / (1.0 + jnp.exp(-gate)) * accu[h]).astype(BF16)

    def down(h, k):
        chip = (x + k) % NX
        cols = pl.ds(pl.multiple_of(chip * 2 * RW, 256), 2 * RW)
        part = jnp.dot(hid[h], wd[:, cols], preferred_element_type=F32).astype(BF16)
        part2[h, k, 0] = part[:, :RW].reshape(8, 32, RW)
        part2[h, k, 1] = part[:, RW:].reshape(8, 32, RW)
        st[h]["pair", k] = remote(part2.at[h, k, 1 - c], mate2.at[h, k], on_tp(mate))

    def down_direct(h):
        part = jnp.dot(hid[h], wd[:, DIRECT:], preferred_element_type=F32).astype(BF16)
        part1[h, 0] = part[:, :DW].reshape(8, 32, DW)
        part1[h, 1] = part[:, DW:].reshape(8, 32, DW)
        st[h]["pair_direct"] = remote(part1.at[h, 1 - c], mate1.at[h], on_tp(mate))

    def chip_sum(h, k, start):
        return part2[h, k, c, start:start + 4].astype(F32) + mate2[h, k, start:start + 4].astype(F32)

    def reduce_far(h):
        st[h]["pair", 2].wait_recv()
        far_s[h, 0] = chip_sum(h, 2, 0).astype(BF16)
        st[h]["far_lo"] = remote(far_s.at[h, 0], far_r.at[h, 0], on_tp(right))
        far_s[h, 1] = chip_sum(h, 2, 4).astype(BF16)
        st[h]["far_hi"] = remote(far_s.at[h, 1], far_r.at[h, 1], on_tp(left))

    def reduce_near_first(h):
        st[h]["pair", 1].wait_recv()
        near_s[h, 0, 1] = chip_sum(h, 1, 4).astype(BF16)
        st[h]["near_r_hi"] = remote(near_s.at[h, 0, 1], near_r.at[h, 0, 1], on_tp(right))
        st[h]["pair", 3].wait_recv()
        near_s[h, 1, 0] = chip_sum(h, 3, 0).astype(BF16)
        st[h]["near_l_lo"] = remote(near_s.at[h, 1, 0], near_r.at[h, 1, 0], on_tp(left))

    def reduce_near_second(h):
        st[h]["far_lo"].wait_recv()
        near_s[h, 0, 0] = (chip_sum(h, 1, 0) + far_r[h, 0].astype(F32)).astype(BF16)
        st[h]["near_r_lo"] = remote(near_s.at[h, 0, 0], near_r.at[h, 0, 0], on_tp(right))
        st[h]["far_hi"].wait_recv()
        near_s[h, 1, 1] = (chip_sum(h, 3, 4) + far_r[h, 1].astype(F32)).astype(BF16)
        st[h]["near_l_hi"] = remote(near_s.at[h, 1, 1], near_r.at[h, 1, 1], on_tp(left))

    back2, back1 = [], []

    def give_back(h, start, stop, fin, landing, copies):
        for j in range(start, stop):
            dy, dz = HOPS[h * 8 + j]
            if dy or dz:
                other = ((y + NY - dy) % NY) * NZ + (z + NZ - dz) % NZ
                copies.append(remote(fin.at[h, j], landing.at[ep], on_ep(other)))
            else:
                landing[ep] = fin[h, j]

    def reduce_last(h):
        s = st[h]
        s["pair", 0].wait_recv()
        arrived([s["near_r_hi"], s["near_l_hi"]])
        total = chip_sum(h, 0, 4) + near_r[h, 0, 1].astype(F32) + near_r[h, 1, 1].astype(F32)
        fin2[h, 4:8] = total.astype(BF16)
        give_back(h, 4, 8, fin2, r2, back2)
        arrived([s["near_r_lo"], s["near_l_lo"]])
        total = chip_sum(h, 0, 0) + near_r[h, 0, 0].astype(F32) + near_r[h, 1, 0].astype(F32)
        fin2[h, 0:4] = total.astype(BF16)
        give_back(h, 0, 4, fin2, r2, back2)

    def direct_back(h):
        st[h]["pair_direct"].wait_recv()
        fin1[h] = (part1[h, c].astype(F32) + mate1[h].astype(F32)).astype(BF16)
        give_back(h, 0, 8, fin1, r1, back1)

    A, B = 0, 1
    LEFT = ("m_left_lo", "m_left_hi")
    RIGHT = ("m_right_lo", "m_right_hi")
    FAR = ("m_far_lo", "m_far_hi")
    with scope("k10_ownA"):
        arrived(of_half(spread2, A))
        own_first(A)
        own_second(A)
    with scope("k11_ownB1"):
        arrived(of_half(spread2, B))
        own_first(B)
        spread1.update(spread(p1, x1.at[c]))
    with scope("k12_guA_own"):
        loads[0].wait()
        loads[1].wait()
        gate_up(A, 0, ("m_own",))
    with scope("k13_fwdA"):
        forward(A)
    with scope("k14_nearA"):
        own_second(B)
        near_rest(A)
    with scope("k15_guB_own"):
        gate_up(B, 0, ("m_own",))
    with scope("k16_fwdB"):
        forward(B)
    with scope("k17_farA"):
        far_rest(A)
    with scope("k18_guA_lr"):
        gate_up(A, 3, LEFT)
        gate_up(A, 1, RIGHT)
    with scope("k19_directA"):
        direct_share(A)
    with scope("k20_guA_far"):
        gate_up(A, 2, FAR)
    with scope("k21_guA_d"):
        gate_up_direct(A)
    with scope("k22_downA21"):
        silu(A)
        loads[2].wait()
        down(A, 2)
        down(A, 1)
    with scope("k23_nearB"):
        near_rest(B)
    with scope("k24_directB"):
        direct_share(B)
    with scope("k25_rfarA"):
        reduce_far(A)
    with scope("k26_downA30d"):
        down(A, 3)
        down(A, 0)
        down_direct(A)
    with scope("k27_rnear1A"):
        reduce_near_first(A)
    with scope("k28_farB"):
        far_rest(B)
    with scope("k29_guB_lr"):
        gate_up(B, 3, LEFT)
        gate_up(B, 1, RIGHT)
    with scope("k30_guB_d"):
        gate_up_direct(B)
    with scope("k31_rnear2A"):
        reduce_near_second(A)
    with scope("k32_dbackA"):
        direct_back(A)
    with scope("k33_guB_far"):
        gate_up(B, 2, FAR)
    with scope("k34_downB21"):
        silu(B)
        down(B, 2)
        down(B, 1)
    with scope("k35_rfarB"):
        reduce_far(B)
    with scope("k36_downB30d"):
        down(B, 3)
        down(B, 0)
        down_direct(B)
    with scope("k37_rnear1B"):
        reduce_near_first(B)
    with scope("k38_rlastA"):
        reduce_last(A)
    with scope("k39_dbackB"):
        direct_back(B)
    with scope("k40_rnear2B"):
        reduce_near_second(B)
    with scope("k41_rlastB"):
        reduce_last(B)

    def weighted(landing, width, out):
        rows = landing[...].reshape(512, width)
        total = jnp.dot(whi[...], rows, preferred_element_type=F32)
        total = total + jnp.dot(wlo[...], rows, preferred_element_type=F32)
        out[...] = total.astype(BF16).reshape(8, 16, width)

    with scope("k42_comb1"):
        arrived(back1)
        weighted(r1, DW, o1s)
        got_o1 = [remote(o1s.at[t], o1r.at[tp], on_tp(t)) for t in peers]
        o1r[tp] = o1s[tp]
    with scope("k44_backwait"):
        arrived(back2)
    with scope("k45_comb2"):
        weighted(r2, RW, o2s)
        got_o2 = [remote(o2s.at[t], o2r.at[tp], on_tp(t)) for t in peers]
        o2r[tp] = o2s[tp]
    with scope("k46_o1"):
        arrived(got_o1)
        for core in range(2):
            total = o1r[core].astype(F32)
            for chip in range(1, NX):
                total = total + o1r[chip * 2 + core].astype(F32)
            out_ref[:, DIRECT + core * DW:DIRECT + (core + 1) * DW] = total.astype(BF16)
    with scope("k47_o2"):
        arrived(got_o2)
    with scope("k48_store"):
        for t in range(8):
            out_ref[:, t * RW:(t + 1) * RW] = o2r[t]
        for copy in sent:
            copy.wait_send()


def body(tokens, routes, combine, gate_weight, up_weight, down_weight):
    info = jnp.concatenate([routes.astype(F32).T, combine.T, jnp.zeros((4, 16), F32)], axis=0)
    info = jnp.tile(info, (1, 8))
    vmem = pl.BlockSpec(memory_space=pltpu.VMEM)
    hbm = pl.BlockSpec(memory_space=pltpu.HBM)
    dma = pltpu.SemaphoreType.DMA
    return pl.pallas_call(
        kernel,
        out_shape=jax.ShapeDtypeStruct((16, 4096), BF16),
        in_specs=[vmem, vmem, hbm, hbm, hbm],
        out_specs=vmem,
        scratch_shapes=[
            pltpu.VMEM((8, 8, 128), F32),
            pltpu.VMEM((8, 16, RW), BF16),
            pltpu.VMEM((8, 16, DW), BF16),
            pltpu.VMEM((16, 32, RW), BF16),
            pltpu.VMEM((16, 32, DW), BF16),
            pltpu.VMEM((8, 2, 8, 32, RW), BF16),
            pltpu.VMEM((2, 2, 8, 32, DW), BF16),
            pltpu.VMEM((4096, 512), BF16),
            pltpu.VMEM((4096, 512), BF16),
            pltpu.VMEM((512, 4096), BF16),
            pltpu.VMEM((2, 256, 512), F32),
            pltpu.VMEM((2, 256, 512), F32),
            pltpu.VMEM((2, 256, 512), BF16),
            pltpu.VMEM((512, 128), BF16),
            pltpu.VMEM((128, 512), BF16),
            pltpu.VMEM((128, 512), BF16),
            pltpu.VMEM((2, 4, 2, 8, 32, RW), BF16),
            pltpu.VMEM((2, 4, 8, 32, RW), BF16),
            pltpu.VMEM((2, 2, 8, 32, DW), BF16),
            pltpu.VMEM((2, 8, 32, DW), BF16),
            pltpu.VMEM((2, 2, 4, 32, RW), BF16),
            pltpu.VMEM((2, 2, 4, 32, RW), BF16),
            pltpu.VMEM((2, 2, 2, 4, 32, RW), BF16),
            pltpu.VMEM((2, 2, 2, 4, 32, RW), BF16),
            pltpu.VMEM((2, 8, 32, RW), BF16),
            pltpu.VMEM((2, 8, 32, DW), BF16),
            pltpu.VMEM((16, 32, RW), BF16),
            pltpu.VMEM((16, 32, DW), BF16),
            pltpu.VMEM((8, 16, RW), BF16),
            pltpu.VMEM((8, 16, DW), BF16),
            pltpu.VMEM((8, 16, RW), BF16),
            pltpu.VMEM((8, 16, DW), BF16),
            dma((3,)),
            dma((COPIES,)),
            dma((COPIES,)),
        ],
        compiler_params=pltpu.CompilerParams(
            collective_id=0, has_side_effects=True, vmem_limit_bytes=60 * 1024 * 1024
        ),
        name="moe",
    )(tokens, info, gate_weight[0], up_weight[0], down_weight[0])


def solution(mesh):
    return jax.shard_map(
        body,
        mesh=mesh,
        in_specs=(
            P(("ep", "tp"), None),
            P(("ep", "tp"), None),
            P(("ep", "tp"), None),
            P("ep", None, "tp"),
            P("ep", None, "tp"),
            P("ep", "tp", None),
        ),
        out_specs=P(("ep", "tp"), None),
        check_vma=False,
    )
```

time: 149 us -> 68.8 us (0.46)
  the two profiles are of different devices: /device:TPU:0 before, /device:TPU:1 now
where the time goes in v2:
time: 68.8 us; the launch traced here: 68.7 us
  Pallas kernels  64.9 us (94%)
  local copies, waits for them, and re-layouts  2.32 us (3%)
  other arithmetic  1.43 us (2%)
    pallas_call x1, Pallas kernels, body(): pl.pallas_call(kernel, out_shape=jax.ShapeDtypeStruct((16, 4096), BF16),...  64.9 us
    unnamed x1, local copies, waits for them, and re-layouts  1.57 us

profile of v2, /device:TPU:1, one launch (start us, length us, event | category | flops | bytes accessed | tf_op | source)
XLA Modules:
  0.0 68.7 jit_solution(5653355717260126262)
XLA Ops:
  0.0 0.1 pad.2.clone
  0.1 0.7 convert_bitcast_fusion
  0.8 0.7 %maximum_maximum_fusion = f32[8,16]{1,0:T(8,128)S(1)} fusion(f32[2,16]{1,0:T(2,128)} %bitcast.9, f32[2,16]{1,0:T(2,128)S(1)} %convert_bitcast_fusion, f32[8]{0:T(128)S(1)} %pad.2.clone), kind=kLoop, calls=%fused_computation | loop fusion | flops 256 | bytes 800 | tf_op jit(solution)/shard_map/concatenate | solution.py:419
  1.5 0.7 tile.10.info_ref
  2.2 64.9 %moe.1 = bf16[16,4096]{1,0:T(8,128)(2,1)} custom-call(bf16[16,4096]{1,0:T(8,128)(2,1)} %tok_ref.1, f32[8,128]{1,0:T(8,128)} %tile.10.info_ref, bf16[4096,512]{1,0:T(8,128)(2,1)} %bitcast.6, bf16[4096,512]{1,0:T(8,128)(2,1)} %bitcast.7, bf16[512,4096]{1,0:T(8,128)(2,1)} %bitcast.8), custom_call_target="tpu_custom_call" | custom-call | tf_op jit(solution)/shard_map/moe/pallas_call | solution.py:424
  67.1 1.6 %copy.8 = bf16[16,4096]{1,0:T(8,128)(2,1)} copy(bf16[16,4096]{1,0:T(8,128)(2,1)} %moe.1) | data formatting | bytes 262144
  (2 shorter events, 0.0 us)

commit v3 on v0

v3 whole, which is shorter than its diff:
```python
from typing import Any, NamedTuple

import jax
import jax.numpy as jnp
from jax import lax
from jax.experimental import pallas as pl
from jax.experimental.pallas import tpu as pltpu
from jax.sharding import PartitionSpec as P

MESH = pl.DeviceIdType.MESH
F32 = jnp.float32
BF16 = jnp.bfloat16
NX, NY, NZ = 4, 4, 4
A, B = 0, 1
RING = (384, 256)
DIRECT = (512, 1024)
RECVS = 57
TALLY = 1024


def hop(h, j):
    dy = j // 2
    return dy, (2 * (j % 2) + dy + h) % NZ


class Half(NamedTuple):
    t2: Any
    t1: Any
    p2: Any
    p1: Any
    x2: Any
    x1: Any
    accg: Any
    accu: Any
    hid: Any
    part2: Any
    mate2: Any
    part1: Any
    mate1: Any
    far_s: Any
    far_r: Any
    near_s: Any
    near_r: Any
    fin2: Any
    fin1: Any
    r2: Any
    r1: Any
    o2s: Any
    o1s: Any
    o2r: Any
    o1r: Any


def half_scratch(h):
    r, d = RING[h], DIRECT[h]
    bf = lambda *shape: pltpu.VMEM(shape, BF16)
    f = lambda *shape: pltpu.VMEM(shape, F32)
    return Half(
        t2=bf(8, 16, r), t1=bf(8, 16, d), p2=bf(8, 32, r), p1=bf(8, 32, d),
        x2=bf(8, 8, 32, r), x1=bf(2, 8, 32, d),
        accg=f(256, 512), accu=f(256, 512), hid=bf(256, 512),
        part2=bf(4, 2, 8, 32, r), mate2=bf(4, 8, 32, r), part1=bf(2, 8, 32, d), mate1=bf(8, 32, d),
        far_s=bf(2, 4, 32, r), far_r=bf(2, 4, 32, r), near_s=bf(2, 2, 4, 32, r), near_r=bf(2, 2, 4, 32, r),
        fin2=bf(8, 32, r), fin1=bf(8, 32, d), r2=bf(8, 32, r), r1=bf(8, 32, d),
        o2s=bf(8, 16, r), o1s=bf(8, 16, d), o2r=bf(8, 16, r), o1r=bf(8, 16, d),
    )


def kernel(
    tok_hbm, routes_hbm, combine_hbm, wg_hbm, wu_hbm, wd_hbm, out_ref,
    tok_ref, routes_ref, combine_ref, info_ref, infos, wg, wu, wd, sel, whi, wlo, tally, expert_of, slot_of, before,
    w_sem, send_sems, recv_sems, *halves,
):
    half = [Half(*halves[:len(Half._fields)]), Half(*halves[len(Half._fields):])]
    ep = lax.axis_index("ep")
    tp = lax.axis_index("tp")
    y, z = ep // NZ, ep % NZ
    x, c = tp // 2, tp % 2
    recv_of = {}
    sent = [0, 0, 0, 0]

    def on_tp(other):
        return {"ep": ep, "tp": other}

    def on_ep(other):
        return {"ep": other, "tp": tp}

    def recv_sem(name):
        return recv_sems.at[recv_of.setdefault(name, len(recv_of))]

    def remote(group, name, src, dst, device):
        size = src.dtype.itemsize
        for dim in src.shape:
            size *= dim
        sent[group] += size // 4096
        pltpu.make_async_remote_copy(
            src_ref=src, dst_ref=dst, send_sem=send_sems.at[group], recv_sem=recv_sem(name),
            device_id=device, device_id_type=MESH,
        ).start()

    def arrived(name, like):
        pltpu.make_async_remote_copy(
            src_ref=like, dst_ref=like, send_sem=send_sems.at[0], recv_sem=recv_sem(name),
            device_id=on_tp(mate), device_id_type=MESH,
        ).wait_recv()

    mate = x * 2 + (1 - c)
    right = ((x + 1) % NX) * 2 + c
    left = ((x + 3) % NX) * 2 + c
    far = ((x + 2) % NX) * 2 + c

    small = []
    for n, (src, dst) in enumerate(
        ((routes_hbm, routes_ref), (combine_hbm, combine_ref), (tok_hbm, tok_ref))
    ):
        load = pltpu.make_async_copy(src, dst, w_sem.at[3 + n])
        load.start()
        small.append(load)
    barrier = pltpu.get_barrier_semaphore()
    for j in range(1, 8):
        pl.semaphore_signal(barrier, inc=1, device_id=on_tp((tp + j) % 8), device_id_type=MESH)
    for dy in range(NY):
        for dz in range(NZ):
            if dy or dz:
                other = ((y + dy) % NY) * NZ + (z + dz) % NZ
                pl.semaphore_signal(barrier, inc=1, device_id=on_ep(other), device_id_type=MESH)
    small[0].wait()
    small[1].wait()
    info_ref[0:2, :] = jnp.concatenate([routes_ref[...].astype(F32)] * 8, axis=1)
    info_ref[2:4, :] = jnp.concatenate([combine_ref[...]] * 8, axis=1)
    info_ref[4:8, :] = jnp.zeros((4, 128), F32)
    small[2].wait()
    pl.semaphore_wait(barrier, 22)

    def ring_cols(h, t):
        return pl.ds(pl.multiple_of(t * RING[h], 128), RING[h])

    def direct_cols(h, core):
        return pl.ds(pl.multiple_of(8 * RING[h] + core * DIRECT[h], 128), DIRECT[h])

    peers = [(tp + j) % 8 for j in (4, 5, 3, 2, 6, 7, 1)]
    for t in peers:
        remote(0, "info", info_ref, infos.at[tp], on_tp(t))
    for h in (A, B):
        for t in peers:
            remote(0, ("t2", h), tok_ref.at[:, ring_cols(h, t)], half[h].t2.at[tp], on_tp(t))
    infos[tp] = info_ref[...]
    for h in (A, B):
        half[h].t2[tp] = tok_ref[:, ring_cols(h, tp)]
        half[h].t1[tp] = tok_ref[:, direct_cols(h, c)]
    loads = []
    for n, (src, dst) in enumerate(((wg_hbm, wg), (wu_hbm, wu), (wd_hbm, wd))):
        load = pltpu.make_async_copy(src, dst, w_sem.at[n])
        load.start()
        loads.append(load)
    row = lax.broadcasted_iota(jnp.int32, (512, 128), 0)
    lane = lax.broadcasted_iota(jnp.int32, (512, 128), 1)
    j_of = (row // 32) % 8
    dy_of = j_of // 2
    dz_of = (2 * (j_of % 2) + dy_of + row // 256) % NZ
    expert_of[...] = (((y + dy_of) % NY) * NZ + (z + dz_of) % NZ).astype(F32)
    same = (lane // 16) == ((row % 32) // 4)
    slot_of[...] = jnp.where(same, row % 4, 128).astype(F32)
    urow = lax.broadcasted_iota(jnp.int32, (128, 128), 0)
    ulane = lax.broadcasted_iota(jnp.int32, (128, 128), 1)
    before[...] = jnp.where((urow < ulane) & ((urow // 16) == (ulane // 16)), 1.0, 0.0).astype(BF16)
    arrived("info", infos.at[pl.ds(0, 7)])
    for h in (A, B):
        for t in peers:
            remote(0, ("t1", h), tok_ref.at[:, direct_cols(h, t % 2)], half[h].t1.at[tp], on_tp(t))

    lane8 = lax.broadcasted_iota(jnp.int32, (8, 128), 1) // 16
    info = jnp.zeros((8, 128), F32)
    for b in range(8):
        info = info + jnp.where(lane8 == b, infos[b], 0.0)
    expert = expert_of[...]
    first_of = jnp.where(info[0:1] == expert, 1.0, 0.0)
    second_of = jnp.where(info[1:2] == expert, 1.0, 0.0)
    named = first_of + second_of
    count = jnp.dot(named.astype(BF16), before[...], preferred_element_type=F32)
    hit = count == slot_of[...]
    sel[...] = jnp.where(hit, named, 0.0).astype(BF16)

    def pick(h, tokens, width, picked, landing, name):
        rows = sel[h * 256:(h + 1) * 256]
        got = jnp.dot(rows, tokens[...].reshape(128, width), preferred_element_type=F32)
        picked[...] = got.astype(BF16).reshape(8, 32, width)
        order = (4, 5, 6, 7, 2, 3, 1, 0) if h == A else (4, 5, 6, 2, 3, 7, 0, 1)
        for j in order:
            dy, dz = hop(h, j)
            if dy or dz:
                other = ((y + dy) % NY) * NZ + (z + dz) % NZ
                remote(0, (name, h), picked.at[j], landing.at[j], on_ep(other))
            else:
                landing[j] = picked[j]

    def others(h):
        return pl.ds(0, 7 if h == A else 8)

    def pick_ring(h):
        arrived(("t2", h), half[h].t2.at[pl.ds(0, 7)])
        pick(h, half[h].t2, RING[h], half[h].p2, half[h].x2.at[tp], "spread2")

    def pick_direct(h):
        arrived(("t1", h), half[h].t1.at[pl.ds(0, 7)])
        pick(h, half[h].t1, DIRECT[h], half[h].p1, half[h].x1.at[c], "spread1")

    pick_ring(A)
    pick_ring(B)
    weight = jnp.where(hit, first_of * info[2:3] + second_of * info[3:4], 0.0).T
    high = weight.astype(BF16)
    whi[...] = high
    wlo[...] = (weight - high.astype(F32)).astype(BF16)

    LO, HI, ALL = pl.ds(0, 4), pl.ds(4, 4), pl.ds(0, 8)

    def push(name, t, h, rows, device):
        block = half[h].x2.at[t, rows]
        remote(1, (name, h), block, block, on_tp(device))

    def got(name, h, rows):
        arrived((name, h), half[h].x2.at[0, rows])

    def own_first(h):
        push("m_own", tp, h, ALL, mate)
        push("r_lo", tp, h, LO, right)
        push("l_hi", tp, h, HI, left)

    def own_second(h):
        push("r_hi", tp, h, HI, right)
        push("l_lo", tp, h, LO, left)

    def forward(h):
        got("r_lo", h, LO)
        push("m_left", left, h, LO, mate)
        push("f_lo", left, h, LO, right)
        got("l_hi", h, HI)
        push("m_right", right, h, HI, mate)
        push("f_hi", right, h, HI, left)

    def near_rest(h):
        got("r_hi", h, HI)
        push("m_left", left, h, HI, mate)
        got("l_lo", h, LO)
        push("m_right", right, h, LO, mate)

    def far_rest(h):
        got("f_lo", h, LO)
        push("m_far", far, h, LO, mate)
        got("f_hi", h, HI)
        push("m_far", far, h, HI, mate)

    def direct_share(h):
        x1 = half[h].x1
        arrived(("spread1", h), x1.at[0, others(h)])
        remote(1, ("m_direct", h), x1.at[c], x1.at[c], on_tp(mate))

    def accumulate(h, a, rows, fresh):
        gate = jnp.dot(a, wg[rows, :], preferred_element_type=F32)
        up = jnp.dot(a, wu[rows, :], preferred_element_type=F32)
        if fresh:
            half[h].accg[...] = gate
            half[h].accu[...] = up
        else:
            half[h].accg[...] += gate
            half[h].accu[...] += up

    def gate_up(h, k, name):
        got(name, h, ALL)
        chip = (x + k) % NX
        x2, r = half[h].x2, RING[h]
        a = jnp.concatenate([x2[chip * 2].reshape(256, r), x2[chip * 2 + 1].reshape(256, r)], axis=1)
        accumulate(h, a, pl.ds(pl.multiple_of(chip * 2 * r, 256), 2 * r), k == 0)

    def gate_up_direct(h):
        x1, d = half[h].x1, DIRECT[h]
        arrived(("m_direct", h), x1.at[0])
        a = jnp.concatenate([x1[0].reshape(256, d), x1[1].reshape(256, d)], axis=1)
        accumulate(h, a, pl.ds(8 * RING[h], 2 * d), False)

    def silu(h):
        gate = half[h].accg[...]
        half[h].hid[...] = (gate / (1.0 + jnp.exp(-gate)) * half[h].accu[...]).astype(BF16)

    def down(h, *ks):
        s, r = half[h], RING[h]
        parts = []
        for k in ks:
            cols = pl.ds(pl.multiple_of(((x + k) % NX) * 2 * r, 256), 2 * r)
            parts.append(jnp.dot(s.hid[...], wd[:, cols], preferred_element_type=F32).astype(BF16))
        for k, part in zip(ks, parts):
            s.part2[k, 0] = part[:, :r].reshape(8, 32, r)
            s.part2[k, 1] = part[:, r:].reshape(8, 32, r)
        for k in ks:
            remote(2, ("pair", h, k), s.part2.at[k, 1 - c], s.mate2.at[k], on_tp(mate))

    def down_direct(h):
        s, d = half[h], DIRECT[h]
        for core in range(2):
            cols = pl.ds(8 * RING[h] + core * d, d)
            part = jnp.dot(s.hid[...], wd[:, cols], preferred_element_type=F32).astype(BF16)
            s.part1[core] = part.reshape(8, 32, d)
        remote(2, ("pair_direct", h), s.part1.at[1 - c], s.mate1, on_tp(mate))

    def paired(h, k):
        arrived(("pair", h, k), half[h].mate2.at[k])

    def chip_sum(h, k, start):
        s = half[h]
        return s.part2[k, c, start:start + 4].astype(F32) + s.mate2[k, start:start + 4].astype(F32)

    def reduce_far(h):
        s = half[h]
        paired(h, 2)
        s.far_s[0] = chip_sum(h, 2, 0).astype(BF16)
        remote(2, ("far_lo", h), s.far_s.at[0], s.far_r.at[0], on_tp(right))
        s.far_s[1] = chip_sum(h, 2, 4).astype(BF16)
        remote(2, ("far_hi", h), s.far_s.at[1], s.far_r.at[1], on_tp(left))

    def near_send(h, side, rows, value):
        s = half[h]
        s.near_s[side, rows] = value.astype(BF16)
        name = ("near_hi" if rows else "near_lo", h)
        remote(2, name, s.near_s.at[side, rows], s.near_r.at[side, rows], on_tp((right, left)[side]))

    def reduce_near_first(h):
        paired(h, 1)
        near_send(h, 0, 1, chip_sum(h, 1, 4))
        paired(h, 3)
        near_send(h, 1, 0, chip_sum(h, 3, 0))

    def reduce_near_second(h):
        s = half[h]
        arrived(("far_lo", h), s.far_r.at[0])
        near_send(h, 0, 0, chip_sum(h, 1, 0) + s.far_r[0].astype(F32))
        arrived(("far_hi", h), s.far_r.at[1])
        near_send(h, 1, 1, chip_sum(h, 3, 4) + s.far_r[1].astype(F32))

    def give_back(h, blocks, fin, landing, name):
        for j in blocks:
            dy, dz = hop(h, j)
            if dy or dz:
                other = ((y + NY - dy) % NY) * NZ + (z + NZ - dz) % NZ
                remote(3, (name, h), fin.at[j], landing.at[j], on_ep(other))
            else:
                landing[j] = fin[j]

    def reduce_last(h):
        s = half[h]
        paired(h, 0)
        near_r = s.near_r
        for rows, name in ((1, "near_hi"), (0, "near_lo")):
            arrived((name, h), near_r.at[0])
            total = chip_sum(h, 0, rows * 4)
            total = total + near_r[0, rows].astype(F32) + near_r[1, rows].astype(F32)
            s.fin2[rows * 4:rows * 4 + 4] = total.astype(BF16)
            give_back(h, range(rows * 4, rows * 4 + 4), s.fin2, s.r2, "back2")

    def direct_back(h):
        s = half[h]
        arrived(("pair_direct", h), s.mate1)
        s.fin1[...] = (s.part1[c].astype(F32) + s.mate1[...].astype(F32)).astype(BF16)
        give_back(h, (4, 5, 6, 7, 2, 3, 0, 1), s.fin1, s.r1, "back1")

    def weigh(h, name, landing, width, out, everywhere):
        arrived((name, h), landing.at[others(h)])
        rows = landing[...].reshape(256, width)
        cols = slice(h * 256, (h + 1) * 256)
        total = jnp.dot(whi[:, cols], rows, preferred_element_type=F32)
        total = total + jnp.dot(wlo[:, cols], rows, preferred_element_type=F32)
        out[...] = total.astype(BF16).reshape(8, 16, width)
        for t in peers:
            remote(3, (name, "out", h), out.at[t], everywhere.at[tp], on_tp(t))
        everywhere[tp] = out[tp]

    def weigh_ring(h):
        weigh(h, "back2", half[h].r2, RING[h], half[h].o2s, half[h].o2r)

    def weigh_direct(h):
        weigh(h, "back1", half[h].r1, DIRECT[h], half[h].o1s, half[h].o1r)

    arrived(("spread2", A), half[A].x2.at[0, others(A)])
    own_first(A)
    own_second(A)
    pick_direct(A)
    pick_direct(B)
    loads[0].wait()
    loads[1].wait()
    gate_up(A, 0, "m_own")
    arrived(("spread2", B), half[B].x2.at[0, others(B)])
    forward(A)
    own_first(B)
    own_second(B)
    near_rest(A)
    gate_up(B, 0, "m_own")
    gate_up(A, 3, "m_left")
    gate_up(A, 1, "m_right")
    direct_share(A)
    far_rest(A)
    forward(B)
    gate_up_direct(A)
    gate_up(A, 2, "m_far")
    silu(A)
    loads[2].wait()
    down(A, 2)
    down_direct(A)
    near_rest(B)
    reduce_far(A)
    down(A, 1, 3)
    direct_share(B)
    gate_up(B, 3, "m_left")
    gate_up(B, 1, "m_right")
    far_rest(B)
    direct_back(A)
    reduce_near_first(A)
    gate_up_direct(B)
    gate_up(B, 2, "m_far")
    silu(B)
    down(B, 2)
    down_direct(B)
    reduce_near_second(A)
    reduce_far(B)
    down(B, 1, 3)
    direct_back(B)
    reduce_near_first(B)
    down(A, 0)
    down(B, 0)
    reduce_near_second(B)
    reduce_last(A)
    reduce_last(B)
    weigh_direct(A)
    weigh_direct(B)
    weigh_ring(A)
    weigh_ring(B)
    totals = []
    for h in (A, B):
        s = half[h]
        arrived(("back1", "out", h), s.o1r.at[pl.ds(0, 7)])
        arrived(("back2", "out", h), s.o2r.at[pl.ds(0, 7)])
    for h in (A, B):
        s = half[h]
        pieces = [s.o2r[t].astype(F32) for t in range(8)]
        for core in range(2):
            piece = s.o1r[core].astype(F32)
            for chip in range(1, NX):
                piece = piece + s.o1r[chip * 2 + core].astype(F32)
            pieces.append(piece)
        totals.append(jnp.concatenate(pieces, axis=1))
    out_ref[...] = (totals[0] + totals[1]).astype(BF16)
    for group in range(4):
        every = tally.at[pl.ds(0, sent[group])]
        pltpu.make_async_remote_copy(
            src_ref=every, dst_ref=every, send_sem=send_sems.at[group], recv_sem=recv_sems.at[0],
            device_id=on_tp(mate), device_id_type=MESH,
        ).wait_send()
    assert len(recv_of) == RECVS, len(recv_of)


def body(tokens, routes, combine, gate_weight, up_weight, down_weight):
    vmem = pl.BlockSpec(memory_space=pltpu.VMEM)
    hbm = pl.BlockSpec(memory_space=pltpu.HBM)
    dma = pltpu.SemaphoreType.DMA
    return pl.pallas_call(
        kernel,
        out_shape=jax.ShapeDtypeStruct((16, 4096), BF16),
        in_specs=[hbm] * 6,
        out_specs=vmem,
        scratch_shapes=[
            pltpu.VMEM((16, 4096), BF16),
            pltpu.VMEM((2, 16), jnp.int32),
            pltpu.VMEM((2, 16), F32),
            pltpu.VMEM((8, 128), F32),
            pltpu.VMEM((8, 8, 128), F32),
            pltpu.VMEM((4096, 512), BF16),
            pltpu.VMEM((4096, 512), BF16),
            pltpu.VMEM((512, 4096), BF16),
            pltpu.VMEM((512, 128), BF16),
            pltpu.VMEM((128, 512), BF16),
            pltpu.VMEM((128, 512), BF16),
            pltpu.VMEM((TALLY, 8, 128), F32),
            pltpu.VMEM((512, 128), F32),
            pltpu.VMEM((512, 128), F32),
            pltpu.VMEM((128, 128), BF16),
            dma((6,)),
            dma((4,)),
            dma((RECVS,)),
            *half_scratch(A),
            *half_scratch(B),
        ],
        compiler_params=pltpu.CompilerParams(
            collective_id=0, has_side_effects=True, vmem_limit_bytes=60 * 1024 * 1024
        ),
        name="moe",
    )(tokens, routes.T, combine.T, gate_weight[0], up_weight[0], down_weight[0])


def solution(mesh):
    return jax.shard_map(
        body,
        mesh=mesh,
        in_specs=(
            P(("ep", "tp"), None),
            P(("ep", "tp"), None),
            P(("ep", "tp"), None),
            P("ep", None, "tp"),
            P("ep", None, "tp"),
            P("ep", "tp", None),
        ),
        out_specs=P(("ep", "tp"), None),
        check_vma=False,
    )
```

time: 149 us -> 59.2 us (0.40)
  the two profiles are of different devices: /device:TPU:0 before, /device:TPU:1 now
where the time goes in v3:
time: 59.2 us; the launch traced here: 59 us
  Pallas kernels  57.4 us (97%)
  local copies, waits for them, and re-layouts  1.57 us (3%)
    pallas_call x1, Pallas kernels, body(): pl.pallas_call(kernel, out_shape=jax.ShapeDtypeStruct((16, 4096), BF16),...  57.4 us
    unnamed x1, local copies, waits for them, and re-layouts  1.57 us

profile of v3, /device:TPU:1, one launch (start us, length us, event | category | flops | bytes accessed | tf_op | source)
XLA Modules:
  0.0 59.0 jit_solution(10152217607910506487)
XLA Ops:
  0.0 57.4 %moe.1 = bf16[16,4096]{1,0:T(8,128)(2,1)} custom-call(bf16[16,4096]{1,0:T(8,128)(2,1)} %tok_hbm.1, s32[2,16]{1,0:T(2,128)} %bitcast.8, f32[2,16]{1,0:T(2,128)} %bitcast.9, bf16[4096,512]{1,0:T(8,128)(2,1)} %bitcast.5, bf16[4096,512]{1,0:T(8,128)(2,1)} %bitcast.6, bf16[512,4096]{1,0:T(8,128)(2,1)} %bitcast.7), custom_call_target="tpu_custom_call" | custom-call | tf_op jit(solution)/shard_map/moe/pallas_call | solution.py:463
  57.4 1.6 %copy.8 = bf16[16,4096]{1,0:T(8,128)(2,1)} copy(bf16[16,4096]{1,0:T(8,128)(2,1)} %moe.1) | data formatting | bytes 262144

commit v4 on v3

--- a/solution.py
+++ b/solution.py
@@ -12,9 +12,9 @@
 BF16 = jnp.bfloat16
 NX, NY, NZ = 4, 4, 4
 A, B = 0, 1
-RING = (384, 256)
-DIRECT = (512, 1024)
-RECVS = 57
+RING = (256, 384)
+DIRECT = (1024, 512)
+RECVS = 59
 TALLY = 1024
 
 
@@ -33,6 +33,7 @@
     accg: Any
     accu: Any
     hid: Any
+    hidp: Any
     part2: Any
     mate2: Any
     part1: Any
@@ -49,6 +50,8 @@
     o1s: Any
     o2r: Any
     o1r: Any
+    w2hi: Any
+    w2lo: Any
 
 
 def half_scratch(h):
@@ -58,17 +61,18 @@
     return Half(
         t2=bf(8, 16, r), t1=bf(8, 16, d), p2=bf(8, 32, r), p1=bf(8, 32, d),
         x2=bf(8, 8, 32, r), x1=bf(2, 8, 32, d),
-        accg=f(256, 512), accu=f(256, 512), hid=bf(256, 512),
-        part2=bf(4, 2, 8, 32, r), mate2=bf(4, 8, 32, r), part1=bf(2, 8, 32, d), mate1=bf(8, 32, d),
+        accg=f(256, 512), accu=f(256, 512), hid=bf(256, 512), hidp=bf(256, 512),
+        part2=bf(2, 4, 4, 64, r), mate2=bf(4, 4, 64, r), part1=bf(2, 8, 32, d), mate1=bf(8, 32, d),
         far_s=bf(2, 4, 32, r), far_r=bf(2, 4, 32, r), near_s=bf(2, 2, 4, 32, r), near_r=bf(2, 2, 4, 32, r),
-        fin2=bf(8, 32, r), fin1=bf(8, 32, d), r2=bf(8, 32, r), r1=bf(8, 32, d),
-        o2s=bf(8, 16, r), o1s=bf(8, 16, d), o2r=bf(8, 16, r), o1r=bf(8, 16, d),
+        fin2=bf(4, 8, 8, r), fin1=bf(8, 32, d), r2=bf(4, 8, 8, r), r1=bf(8, 32, d),
+        o2s=bf(2, 4, 16, r), o1s=bf(8, 16, d), o2r=bf(4, 16, r), o1r=bf(8, 16, d),
+        w2hi=bf(32, 64), w2lo=bf(32, 64),
     )
 
 
 def kernel(
     tok_hbm, routes_hbm, combine_hbm, wg_hbm, wu_hbm, wd_hbm, out_ref,
-    tok_ref, routes_ref, combine_ref, info_ref, infos, wg, wu, wd, sel, whi, wlo, tally, expert_of, slot_of, before,
+    tok_ref, routes_ref, combine_ref, info_ref, infos, wg, wu, wd, sel, whi, wlo, tally, expert_of, slot_of, before, perm, wrows, wcols, total_ref,
     w_sem, send_sems, recv_sems, *halves,
 ):
     half = [Half(*halves[:len(Half._fields)]), Half(*halves[len(Half._fields):])]
@@ -163,6 +167,11 @@
     slot_of[...] = jnp.where(same, row % 4, 128).astype(F32)
     urow = lax.broadcasted_iota(jnp.int32, (128, 128), 0)
     ulane = lax.broadcasted_iota(jnp.int32, (128, 128), 1)
+    total_ref[...] = jnp.zeros((16, 4096), F32)
+    to = lax.broadcasted_iota(jnp.int32, (256, 256), 0)
+    come = lax.broadcasted_iota(jnp.int32, (256, 256), 1)
+    home = (x + to // 64) % NX
+    perm[...] = jnp.where(come == ((to % 64) // 8) * 32 + home * 8 + to % 8, 1.0, 0.0).astype(BF16)
     before[...] = jnp.where((urow < ulane) & ((urow // 16) == (ulane // 16)), 1.0, 0.0).astype(BF16)
     arrived("info", infos.at[pl.ds(0, 7)])
     for h in (A, B):
@@ -207,10 +216,19 @@
 
     pick_ring(A)
     pick_ring(B)
-    weight = jnp.where(hit, first_of * info[2:3] + second_of * info[3:4], 0.0).T
+    weight = jnp.where(hit, first_of * info[2:3] + second_of * info[3:4], 0.0)
+    wrows[...] = weight.reshape(16, 32, 128)
+    weight = weight.T
     high = weight.astype(BF16)
     whi[...] = high
     wlo[...] = (weight - high.astype(F32)).astype(BF16)
+    wcols[...] = wrows[:, pl.ds(pl.multiple_of(x * 8, 8), 8), :].reshape(128, 128).T
+    mine = wcols[pl.ds(pl.multiple_of(x * 32, 32), 32), :]
+    for h in (A, B):
+        part = mine[:, h * 64:(h + 1) * 64]
+        high = part.astype(BF16)
+        half[h].w2hi[...] = high
+        half[h].w2lo[...] = (part - high.astype(F32)).astype(BF16)
 
     LO, HI, ALL = pl.ds(0, 4), pl.ds(4, 4), pl.ds(0, 8)
 
@@ -272,27 +290,39 @@
         a = jnp.concatenate([x2[chip * 2].reshape(256, r), x2[chip * 2 + 1].reshape(256, r)], axis=1)
         accumulate(h, a, pl.ds(pl.multiple_of(chip * 2 * r, 256), 2 * r), k == 0)
 
-    def gate_up_direct(h):
-        x1, d = half[h].x1, DIRECT[h]
-        arrived(("m_direct", h), x1.at[0])
-        a = jnp.concatenate([x1[0].reshape(256, d), x1[1].reshape(256, d)], axis=1)
-        accumulate(h, a, pl.ds(8 * RING[h], 2 * d), False)
+    def gate_up_part(h, k, core, name):
+        if name is not None:
+            got(name, h, ALL)
+        t = ((x + k) % NX) * 2 + core
+        r = RING[h]
+        accumulate(h, half[h].x2[t].reshape(256, r), ring_cols(h, t), False)
+
+    def gate_up_direct_own(h):
+        accumulate(h, half[h].x1[c].reshape(256, DIRECT[h]), direct_cols(h, c), False)
+
+    def gate_up_direct_mate(h):
+        arrived(("m_direct", h), half[h].x1.at[0])
+        accumulate(h, half[h].x1[1 - c].reshape(256, DIRECT[h]), direct_cols(h, 1 - c), False)
 
     def silu(h):
         gate = half[h].accg[...]
         half[h].hid[...] = (gate / (1.0 + jnp.exp(-gate)) * half[h].accu[...]).astype(BF16)
-
-    def down(h, *ks):
+        half[h].hidp[...] = jnp.dot(perm[...], half[h].hid[...], preferred_element_type=F32).astype(BF16)
+
+    def down(h, g):
         s, r = half[h], RING[h]
         parts = []
-        for k in ks:
-            cols = pl.ds(pl.multiple_of(((x + k) % NX) * 2 * r, 256), 2 * r)
-            parts.append(jnp.dot(s.hid[...], wd[:, cols], preferred_element_type=F32).astype(BF16))
-        for k, part in zip(ks, parts):
-            s.part2[k, 0] = part[:, :r].reshape(8, 32, r)
-            s.part2[k, 1] = part[:, r:].reshape(8, 32, r)
-        for k in ks:
-            remote(2, ("pair", h, k), s.part2.at[k, 1 - c], s.mate2.at[k], on_tp(mate))
+        for m in (2 * g, 2 * g + 1):
+            cols = pl.ds(m * 2 * r, 2 * r)
+            parts.append(jnp.dot(s.hidp[...], wd[:, cols], preferred_element_type=F32).astype(BF16))
+        for m, part in zip((2 * g, 2 * g + 1), parts):
+            for core in range(2):
+                s.part2[core, :, m] = part[:, core * r:(core + 1) * r].reshape(4, 64, r)
+        chunks = pl.ds(2 * g, 2)
+        remote(2, ("far", h, g), s.part2.at[1 - c, 2, chunks], s.mate2.at[2, chunks], on_tp(mate))
+        if g:
+            for k in (1, 3, 0):
+                remote(2, ("pair", h, k), s.part2.at[1 - c, k], s.mate2.at[k], on_tp(mate))
 
     def down_direct(h):
         s, d = half[h], DIRECT[h]
@@ -305,17 +335,18 @@
     def paired(h, k):
         arrived(("pair", h, k), half[h].mate2.at[k])
 
-    def chip_sum(h, k, start):
-        s = half[h]
-        return s.part2[k, c, start:start + 4].astype(F32) + s.mate2[k, start:start + 4].astype(F32)
-
-    def reduce_far(h):
-        s = half[h]
-        paired(h, 2)
-        s.far_s[0] = chip_sum(h, 2, 0).astype(BF16)
-        remote(2, ("far_lo", h), s.far_s.at[0], s.far_r.at[0], on_tp(right))
-        s.far_s[1] = chip_sum(h, 2, 4).astype(BF16)
-        remote(2, ("far_hi", h), s.far_s.at[1], s.far_r.at[1], on_tp(left))
+    def chip_sum(h, k, rows, chunks=slice(None)):
+        s = half[h]
+        rows = pl.ds(rows * 32, 32)
+        return s.part2[c, k, chunks, rows, :].astype(F32) + s.mate2[k, chunks, rows, :].astype(F32)
+
+    def reduce_far(h, g):
+        s = half[h]
+        chunks = pl.ds(2 * g, 2)
+        arrived(("far", h, g), s.mate2.at[2, chunks])
+        for rows, name, device in ((0, "far_lo", right), (1, "far_hi", left)):
+            s.far_s[rows, chunks] = chip_sum(h, 2, rows, chunks).astype(BF16)
+            remote(2, (name, h), s.far_s.at[rows, chunks], s.far_r.at[rows, chunks], on_tp(device))
 
     def near_send(h, side, rows, value):
         s = half[h]
@@ -325,7 +356,7 @@
 
     def reduce_near_first(h):
         paired(h, 1)
-        near_send(h, 0, 1, chip_sum(h, 1, 4))
+        near_send(h, 0, 1, chip_sum(h, 1, 1))
         paired(h, 3)
         near_send(h, 1, 0, chip_sum(h, 3, 0))
 
@@ -334,16 +365,17 @@
         arrived(("far_lo", h), s.far_r.at[0])
         near_send(h, 0, 0, chip_sum(h, 1, 0) + s.far_r[0].astype(F32))
         arrived(("far_hi", h), s.far_r.at[1])
-        near_send(h, 1, 1, chip_sum(h, 3, 4) + s.far_r[1].astype(F32))
+        near_send(h, 1, 1, chip_sum(h, 3, 1) + s.far_r[1].astype(F32))
 
     def give_back(h, blocks, fin, landing, name):
         for j in blocks:
+            at = (slice(None), j) if name == "back2" else (j,)
             dy, dz = hop(h, j)
             if dy or dz:
                 other = ((y + NY - dy) % NY) * NZ + (z + NZ - dz) % NZ
-                remote(3, (name, h), fin.at[j], landing.at[j], on_ep(other))
+                remote(3, (name, h), fin.at[at], landing.at[at], on_ep(other))
             else:
-                landing[j] = fin[j]
+                landing[at] = fin[at]
 
     def reduce_last(h):
         s = half[h]
@@ -351,9 +383,9 @@
         near_r = s.near_r
         for rows, name in ((1, "near_hi"), (0, "near_lo")):
             arrived((name, h), near_r.at[0])
-            total = chip_sum(h, 0, rows * 4)
+            total = chip_sum(h, 0, rows)
             total = total + near_r[0, rows].astype(F32) + near_r[1, rows].astype(F32)
-            s.fin2[rows * 4:rows * 4 + 4] = total.astype(BF16)
+            s.fin2[:, rows * 4:rows * 4 + 4] = total.reshape(4, 4, 8, RING[h]).astype(BF16)
             give_back(h, range(rows * 4, rows * 4 + 4), s.fin2, s.r2, "back2")
 
     def direct_back(h):
@@ -362,28 +394,51 @@
         s.fin1[...] = (s.part1[c].astype(F32) + s.mate1[...].astype(F32)).astype(BF16)
         give_back(h, (4, 5, 6, 7, 2, 3, 0, 1), s.fin1, s.r1, "back1")
 
-    def weigh(h, name, landing, width, out, everywhere):
-        arrived((name, h), landing.at[others(h)])
-        rows = landing[...].reshape(256, width)
+    def weigh_ring(h):
+        s, r = half[h], RING[h]
+        arrived(("back2", h), s.r2.at[:, others(h)])
+        for m in range(NX):
+            rows = s.r2[m].astype(F32).reshape(64, r).astype(BF16)
+            total = jnp.dot(s.w2hi[...], rows, preferred_element_type=F32)
+            total = total + jnp.dot(s.w2lo[...], rows, preferred_element_type=F32)
+            s.o2s[:, m] = total.astype(BF16).reshape(2, 16, r)
+        remote(3, ("out2", h), s.o2s.at[1 - c], s.o2r, on_tp(mate))
+
+    def weigh_direct(h):
+        s, d = half[h], DIRECT[h]
+        arrived(("back1", h), s.r1.at[others(h)])
+        rows = s.r1[...].reshape(256, d)
         cols = slice(h * 256, (h + 1) * 256)
         total = jnp.dot(whi[:, cols], rows, preferred_element_type=F32)
         total = total + jnp.dot(wlo[:, cols], rows, preferred_element_type=F32)
-        out[...] = total.astype(BF16).reshape(8, 16, width)
+        s.o1s[...] = total.astype(BF16).reshape(8, 16, d)
         for t in peers:
-            remote(3, (name, "out", h), out.at[t], everywhere.at[tp], on_tp(t))
-        everywhere[tp] = out[tp]
-
-    def weigh_ring(h):
-        weigh(h, "back2", half[h].r2, RING[h], half[h].o2s, half[h].o2r)
-
-    def weigh_direct(h):
-        weigh(h, "back1", half[h].r1, DIRECT[h], half[h].o1s, half[h].o1r)
+            remote(3, ("out1", h), s.o1s.at[t], s.o1r.at[tp], on_tp(t))
+        s.o1r[tp] = s.o1s[tp]
+
+    def put(cols, value):
+        total_ref[:, cols] += value
+
+    def finish_direct(h):
+        s, d = half[h], DIRECT[h]
+        arrived(("out1", h), s.o1r.at[pl.ds(0, 7)])
+        for core in range(2):
+            piece = s.o1r[core].astype(F32)
+            for chip in range(1, NX):
+                piece = piece + s.o1r[chip * 2 + core].astype(F32)
+            put(pl.ds(8 * RING[h] + core * d, d), piece)
+
+    def finish_ring(h):
+        s = half[h]
+        arrived(("out2", h), s.o2r)
+        for m in range(NX):
+            put(ring_cols(h, 2 * m + c), s.o2s[c, m].astype(F32))
+            put(ring_cols(h, 2 * m + 1 - c), s.o2r[m].astype(F32))
 
     arrived(("spread2", A), half[A].x2.at[0, others(A)])
     own_first(A)
     own_second(A)
     pick_direct(A)
-    pick_direct(B)
     loads[0].wait()
     loads[1].wait()
     gate_up(A, 0, "m_own")
@@ -391,62 +446,57 @@
     forward(A)
     own_first(B)
     own_second(B)
+    pick_direct(B)
     near_rest(A)
-    gate_up(B, 0, "m_own")
     gate_up(A, 3, "m_left")
     gate_up(A, 1, "m_right")
+    gate_up(B, 0, "m_own")
+    far_rest(A)
+    gate_up_part(A, 2, c, None)
     direct_share(A)
-    far_rest(A)
+    gate_up_direct_own(A)
+    gate_up_part(A, 2, 1 - c, "m_far")
     forward(B)
-    gate_up_direct(A)
-    gate_up(A, 2, "m_far")
+    near_rest(B)
+    gate_up_direct_mate(A)
     silu(A)
     loads[2].wait()
-    down(A, 2)
-    down_direct(A)
-    near_rest(B)
-    reduce_far(A)
-    down(A, 1, 3)
+    down(A, 0)
+    down(A, 1)
     direct_share(B)
     gate_up(B, 3, "m_left")
+    reduce_far(A, 0)
+    reduce_far(A, 1)
     gate_up(B, 1, "m_right")
+    reduce_near_first(A)
     far_rest(B)
+    down_direct(A)
+    gate_up_direct_own(B)
+    gate_up(B, 2, "m_far")
+    gate_up_direct_mate(B)
+    silu(B)
+    down(B, 0)
+    reduce_near_second(A)
     direct_back(A)
-    reduce_near_first(A)
-    gate_up_direct(B)
-    gate_up(B, 2, "m_far")
-    silu(B)
-    down(B, 2)
+    down(B, 1)
+    reduce_far(B, 0)
+    reduce_far(B, 1)
     down_direct(B)
-    reduce_near_second(A)
-    reduce_far(B)
-    down(B, 1, 3)
+    reduce_near_first(B)
     direct_back(B)
-    reduce_near_first(B)
-    down(A, 0)
-    down(B, 0)
+    reduce_last(A)
     reduce_near_second(B)
-    reduce_last(A)
     reduce_last(B)
     weigh_direct(A)
     weigh_direct(B)
     weigh_ring(A)
+    finish_ring(A)
     weigh_ring(B)
-    totals = []
-    for h in (A, B):
-        s = half[h]
-        arrived(("back1", "out", h), s.o1r.at[pl.ds(0, 7)])
-        arrived(("back2", "out", h), s.o2r.at[pl.ds(0, 7)])
-    for h in (A, B):
-        s = half[h]
-        pieces = [s.o2r[t].astype(F32) for t in range(8)]
-        for core in range(2):
-            piece = s.o1r[core].astype(F32)
-            for chip in range(1, NX):
-                piece = piece + s.o1r[chip * 2 + core].astype(F32)
-            pieces.append(piece)
-        totals.append(jnp.concatenate(pieces, axis=1))
-    out_ref[...] = (totals[0] + totals[1]).astype(BF16)
+    finish_ring(B)
+    finish_direct(A)
+    finish_direct(B)
+    pass
+    out_ref[...] = total_ref[...].astype(BF16)
     for group in range(4):
         every = tally.at[pl.ds(0, sent[group])]
         pltpu.make_async_remote_copy(
@@ -481,6 +531,10 @@
             pltpu.VMEM((512, 128), F32),
             pltpu.VMEM((512, 128), F32),
             pltpu.VMEM((128, 128), BF16),
+            pltpu.VMEM((256, 256), BF16),
+            pltpu.VMEM((16, 32, 128), F32),
+            pltpu.VMEM((128, 128), F32),
+            pltpu.VMEM((16, 4096), F32),
             dma((6,)),
             dma((4,)),
             dma((RECVS,)),

time: 59.2 us -> 56.1 us (0.948)
  Pallas kernels: 57.4 us -> 54.3 us
    pallas_call x1, Pallas kernels: 57.4 us -> 54.3 us  [body(): pl.pallas_call(kernel, out_shape=jax.ShapeDtypeStruct((16, 4096), BF16),...]
where the time goes in v4:
time: 56.1 us; the launch traced here: 55.9 us
  Pallas kernels  54.3 us (97%)
  local copies, waits for them, and re-layouts  1.57 us (3%)
    pallas_call x1, Pallas kernels, body(): pl.pallas_call(kernel, out_shape=jax.ShapeDtypeStruct((16, 4096), BF16),...  54.3 us
    unnamed x1, local copies, waits for them, and re-layouts  1.57 us

profile of v4, /device:TPU:1, one launch (start us, length us, event | category | flops | bytes accessed | tf_op | source)
XLA Modules:
  0.0 55.9 jit_solution(10722148589981351295)
XLA Ops:
  0.0 54.3 %moe.1 = bf16[16,4096]{1,0:T(8,128)(2,1)} custom-call(bf16[16,4096]{1,0:T(8,128)(2,1)} %tok_hbm.1, s32[2,16]{1,0:T(2,128)} %bitcast.8, f32[2,16]{1,0:T(2,128)} %bitcast.9, bf16[4096,512]{1,0:T(8,128)(2,1)} %bitcast.5, bf16[4096,512]{1,0:T(8,128)(2,1)} %bitcast.6, bf16[512,4096]{1,0:T(8,128)(2,1)} %bitcast.7), custom_call_target="tpu_custom_call" | custom-call | tf_op jit(solution)/shard_map/moe/pallas_call | solution.py:513
  54.4 1.6 %copy.8 = bf16[16,4096]{1,0:T(8,128)(2,1)} copy(bf16[16,4096]{1,0:T(8,128)(2,1)} %moe.1) | data formatting | bytes 262144

commit v5 on v4

--- a/solution.py
+++ b/solution.py
@@ -14,7 +14,7 @@
 A, B = 0, 1
 RING = (256, 384)
 DIRECT = (1024, 512)
-RECVS = 59
+RECVS = 63
 TALLY = 1024
 
 
@@ -148,6 +148,8 @@
     for h in (A, B):
         for t in peers:
             remote(0, ("t2", h), tok_ref.at[:, ring_cols(h, t)], half[h].t2.at[tp], on_tp(t))
+    for t in peers:
+        remote(0, ("t1", A), tok_ref.at[:, direct_cols(A, t % 2)], half[A].t1.at[tp], on_tp(t))
     infos[tp] = info_ref[...]
     for h in (A, B):
         half[h].t2[tp] = tok_ref[:, ring_cols(h, tp)]
@@ -174,9 +176,8 @@
     perm[...] = jnp.where(come == ((to % 64) // 8) * 32 + home * 8 + to % 8, 1.0, 0.0).astype(BF16)
     before[...] = jnp.where((urow < ulane) & ((urow // 16) == (ulane // 16)), 1.0, 0.0).astype(BF16)
     arrived("info", infos.at[pl.ds(0, 7)])
-    for h in (A, B):
-        for t in peers:
-            remote(0, ("t1", h), tok_ref.at[:, direct_cols(h, t % 2)], half[h].t1.at[tp], on_tp(t))
+    for t in peers:
+        remote(0, ("t1", B), tok_ref.at[:, direct_cols(B, t % 2)], half[B].t1.at[tp], on_tp(t))
 
     lane8 = lax.broadcasted_iota(jnp.int32, (8, 128), 1) // 16
     info = jnp.zeros((8, 128), F32)
@@ -346,13 +347,14 @@
         arrived(("far", h, g), s.mate2.at[2, chunks])
         for rows, name, device in ((0, "far_lo", right), (1, "far_hi", left)):
             s.far_s[rows, chunks] = chip_sum(h, 2, rows, chunks).astype(BF16)
-            remote(2, (name, h), s.far_s.at[rows, chunks], s.far_r.at[rows, chunks], on_tp(device))
-
-    def near_send(h, side, rows, value):
-        s = half[h]
-        s.near_s[side, rows] = value.astype(BF16)
+            remote(2, (name, h, g), s.far_s.at[rows, chunks], s.far_r.at[rows, chunks], on_tp(device))
+
+    def near_send(h, side, rows, value, chunks=pl.ds(0, 4)):
+        s = half[h]
+        s.near_s[side, rows, chunks] = value.astype(BF16)
         name = ("near_hi" if rows else "near_lo", h)
-        remote(2, name, s.near_s.at[side, rows], s.near_r.at[side, rows], on_tp((right, left)[side]))
+        at = (side, rows, chunks)
+        remote(2, name, s.near_s.at[at], s.near_r.at[at], on_tp((right, left)[side]))
 
     def reduce_near_first(h):
         paired(h, 1)
@@ -360,12 +362,13 @@
         paired(h, 3)
         near_send(h, 1, 0, chip_sum(h, 3, 0))
 
-    def reduce_near_second(h):
-        s = half[h]
-        arrived(("far_lo", h), s.far_r.at[0])
-        near_send(h, 0, 0, chip_sum(h, 1, 0) + s.far_r[0].astype(F32))
-        arrived(("far_hi", h), s.far_r.at[1])
-        near_send(h, 1, 1, chip_sum(h, 3, 1) + s.far_r[1].astype(F32))
+    def reduce_near_second(h, g):
+        s = half[h]
+        chunks = pl.ds(2 * g, 2)
+        arrived(("far_lo", h, g), s.far_r.at[0, chunks])
+        near_send(h, 0, 0, chip_sum(h, 1, 0, chunks) + s.far_r[0, chunks].astype(F32), chunks)
+        arrived(("far_hi", h, g), s.far_r.at[1, chunks])
+        near_send(h, 1, 1, chip_sum(h, 3, 1, chunks) + s.far_r[1, chunks].astype(F32), chunks)
 
     def give_back(h, blocks, fin, landing, name):
         for j in blocks:
@@ -435,10 +438,10 @@
             put(ring_cols(h, 2 * m + c), s.o2s[c, m].astype(F32))
             put(ring_cols(h, 2 * m + 1 - c), s.o2r[m].astype(F32))
 
+    pick_direct(A)
     arrived(("spread2", A), half[A].x2.at[0, others(A)])
     own_first(A)
     own_second(A)
-    pick_direct(A)
     loads[0].wait()
     loads[1].wait()
     gate_up(A, 0, "m_own")
@@ -452,46 +455,49 @@
     gate_up(A, 1, "m_right")
     gate_up(B, 0, "m_own")
     far_rest(A)
+    direct_share(A)
     gate_up_part(A, 2, c, None)
-    direct_share(A)
     gate_up_direct_own(A)
     gate_up_part(A, 2, 1 - c, "m_far")
     forward(B)
-    near_rest(B)
     gate_up_direct_mate(A)
+    direct_share(B)
     silu(A)
     loads[2].wait()
     down(A, 0)
     down(A, 1)
-    direct_share(B)
-    gate_up(B, 3, "m_left")
+    near_rest(B)
+    down_direct(A)
     reduce_far(A, 0)
     reduce_far(A, 1)
+    gate_up_direct_own(B)
+    gate_up_direct_mate(B)
+    far_rest(B)
+    reduce_near_first(A)
+    gate_up(B, 3, "m_left")
     gate_up(B, 1, "m_right")
-    reduce_near_first(A)
-    far_rest(B)
-    down_direct(A)
-    gate_up_direct_own(B)
-    gate_up(B, 2, "m_far")
-    gate_up_direct_mate(B)
+    direct_back(A)
+    gate_up_part(B, 2, c, None)
+    gate_up_part(B, 2, 1 - c, "m_far")
     silu(B)
     down(B, 0)
-    reduce_near_second(A)
-    direct_back(A)
+    reduce_near_second(A, 0)
+    reduce_near_second(A, 1)
     down(B, 1)
     reduce_far(B, 0)
     reduce_far(B, 1)
+    reduce_near_first(B)
     down_direct(B)
-    reduce_near_first(B)
     direct_back(B)
     reduce_last(A)
-    reduce_near_second(B)
+    reduce_near_second(B, 0)
+    reduce_near_second(B, 1)
     reduce_last(B)
     weigh_direct(A)
     weigh_direct(B)
     weigh_ring(A)
+    weigh_ring(B)
     finish_ring(A)
-    weigh_ring(B)
     finish_ring(B)
     finish_direct(A)
     finish_direct(B)

time: 56.1 us -> 54.8 us (0.977)
  Pallas kernels: 54.3 us -> 53.1 us
    pallas_call x1, Pallas kernels: 54.3 us -> 53.1 us  [body(): pl.pallas_call(kernel, out_shape=jax.ShapeDtypeStruct((16, 4096), BF16),...]
where the time goes in v5:
time: 54.8 us; the launch traced here: 54.7 us
  Pallas kernels  53.1 us (97%)
  local copies, waits for them, and re-layouts  1.57 us (3%)
    pallas_call x1, Pallas kernels, body(): pl.pallas_call(kernel, out_shape=jax.ShapeDtypeStruct((16, 4096), BF16),...  53.1 us
    unnamed x1, local copies, waits for them, and re-layouts  1.57 us

profile of v5, /device:TPU:1, one launch (start us, length us, event | category | flops | bytes accessed | tf_op | source)
XLA Modules:
  0.0 54.7 jit_solution(7728392505357816751)
XLA Ops:
  0.0 53.1 %moe.1 = bf16[16,4096]{1,0:T(8,128)(2,1)} custom-call(bf16[16,4096]{1,0:T(8,128)(2,1)} %tok_hbm.1, s32[2,16]{1,0:T(2,128)} %bitcast.8, f32[2,16]{1,0:T(2,128)} %bitcast.9, bf16[4096,512]{1,0:T(8,128)(2,1)} %bitcast.5, bf16[4096,512]{1,0:T(8,128)(2,1)} %bitcast.6, bf16[512,4096]{1,0:T(8,128)(2,1)} %bitcast.7), custom_call_target="tpu_custom_call" | custom-call | tf_op jit(solution)/shard_map/moe/pallas_call | solution.py:519
  53.1 1.6 %copy.8 = bf16[16,4096]{1,0:T(8,128)(2,1)} copy(bf16[16,4096]{1,0:T(8,128)(2,1)} %moe.1) | data formatting | bytes 262144

commit v6 on v5

--- a/solution.py
+++ b/solution.py
@@ -380,12 +380,13 @@
             else:
                 landing[at] = fin[at]
 
-    def reduce_last(h):
-        s = half[h]
-        paired(h, 0)
+    def reduce_last(h, parts):
+        s = half[h]
+        if 1 in parts:
+            paired(h, 0)
         near_r = s.near_r
-        for rows, name in ((1, "near_hi"), (0, "near_lo")):
-            arrived((name, h), near_r.at[0])
+        for rows in parts:
+            arrived(("near_hi" if rows else "near_lo", h), near_r.at[0])
             total = chip_sum(h, 0, rows)
             total = total + near_r[0, rows].astype(F32) + near_r[1, rows].astype(F32)
             s.fin2[:, rows * 4:rows * 4 + 4] = total.reshape(4, 4, 8, RING[h]).astype(BF16)
@@ -489,11 +490,12 @@
     reduce_near_first(B)
     down_direct(B)
     direct_back(B)
-    reduce_last(A)
+    reduce_last(A, (1, 0))
     reduce_near_second(B, 0)
     reduce_near_second(B, 1)
-    reduce_last(B)
+    reduce_last(B, (1,))
     weigh_direct(A)
+    reduce_last(B, (0,))
     weigh_direct(B)
     weigh_ring(A)
     weigh_ring(B)

time: 54.8 us -> 54.8 us (level)
  no operation moved by 1% of the time
where the time goes in v6:
time: 54.8 us; the launch traced here: 54.7 us
  Pallas kernels  53.1 us (97%)
  local copies, waits for them, and re-layouts  1.57 us (3%)
    pallas_call x1, Pallas kernels, body(): pl.pallas_call(kernel, out_shape=jax.ShapeDtypeStruct((16, 4096), BF16),...  53.1 us
    unnamed x1, local copies, waits for them, and re-layouts  1.57 us

profile of v6, /device:TPU:1, one launch (start us, length us, event | category | flops | bytes accessed | tf_op | source)
XLA Modules:
  0.0 54.7 jit_solution(13090672475306725101)
XLA Ops:
  0.0 53.1 %moe.1 = bf16[16,4096]{1,0:T(8,128)(2,1)} custom-call(bf16[16,4096]{1,0:T(8,128)(2,1)} %tok_hbm.1, s32[2,16]{1,0:T(2,128)} %bitcast.8, f32[2,16]{1,0:T(2,128)} %bitcast.9, bf16[4096,512]{1,0:T(8,128)(2,1)} %bitcast.5, bf16[4096,512]{1,0:T(8,128)(2,1)} %bitcast.6, bf16[512,4096]{1,0:T(8,128)(2,1)} %bitcast.7), custom_call_target="tpu_custom_call" | custom-call | tf_op jit(solution)/shard_map/moe/pallas_call | solution.py:521
  53.1 1.6 %copy.8 = bf16[16,4096]{1,0:T(8,128)(2,1)} copy(bf16[16,4096]{1,0:T(8,128)(2,1)} %moe.1) | data formatting | bytes 262144

commit v7 on v5

--- a/solution.py
+++ b/solution.py
@@ -410,13 +410,15 @@
     def weigh_direct(h):
         s, d = half[h], DIRECT[h]
         arrived(("back1", h), s.r1.at[others(h)])
-        rows = s.r1[...].reshape(256, d)
         cols = slice(h * 256, (h + 1) * 256)
-        total = jnp.dot(whi[:, cols], rows, preferred_element_type=F32)
-        total = total + jnp.dot(wlo[:, cols], rows, preferred_element_type=F32)
-        s.o1s[...] = total.astype(BF16).reshape(8, 16, d)
-        for t in peers:
-            remote(3, ("out1", h), s.o1s.at[t], s.o1r.at[tp], on_tp(t))
+        for start in range(0, d, 512):
+            wide = pl.ds(start, 512)
+            rows = s.r1[:, :, wide].reshape(256, 512)
+            total = jnp.dot(whi[:, cols], rows, preferred_element_type=F32)
+            total = total + jnp.dot(wlo[:, cols], rows, preferred_element_type=F32)
+            s.o1s[:, :, wide] = total.astype(BF16).reshape(8, 16, 512)
+            for t in peers:
+                remote(3, ("out1", h), s.o1s.at[t, :, wide], s.o1r.at[tp, :, wide], on_tp(t))
         s.o1r[tp] = s.o1s[tp]
 
     def put(cols, value):

time: 54.8 us -> 54.8 us (level)
  no operation moved by 1% of the time
where the time goes in v7:
time: 54.8 us; the launch traced here: 54.7 us
  Pallas kernels  53.1 us (97%)
  local copies, waits for them, and re-layouts  1.57 us (3%)
    pallas_call x1, Pallas kernels, body(): pl.pallas_call(kernel, out_shape=jax.ShapeDtypeStruct((16, 4096), BF16),...  53.1 us
    unnamed x1, local copies, waits for them, and re-layouts  1.57 us

profile of v7, /device:TPU:1, one launch (start us, length us, event | category | flops | bytes accessed | tf_op | source)
XLA Modules:
  0.0 54.7 jit_solution(11155968458181076220)
XLA Ops:
  0.0 53.1 %moe.1 = bf16[16,4096]{1,0:T(8,128)(2,1)} custom-call(bf16[16,4096]{1,0:T(8,128)(2,1)} %tok_hbm.1, s32[2,16]{1,0:T(2,128)} %bitcast.8, f32[2,16]{1,0:T(2,128)} %bitcast.9, bf16[4096,512]{1,0:T(8,128)(2,1)} %bitcast.5, bf16[4096,512]{1,0:T(8,128)(2,1)} %bitcast.6, bf16[512,4096]{1,0:T(8,128)(2,1)} %bitcast.7), custom_call_target="tpu_custom_call" | custom-call | tf_op jit(solution)/shard_map/moe/pallas_call | solution.py:521
  53.1 1.6 %copy.8 = bf16[16,4096]{1,0:T(8,128)(2,1)} copy(bf16[16,4096]{1,0:T(8,128)(2,1)} %moe.1) | data formatting | bytes 262144
